TPU v7x, 32 devices: a whole 2x2x4 slice. The times are simulated.
32 devices in a mesh: clips: 2 (over x), tm: 4 (over y, core), height: 4 (over z).
Axes of the slice: x: 2, y: 2, z: 4, core: 2. Of those that a mesh axis runs over, the one named last changes fastest.
Arguments:
- features: bfloat16 [16, 16, 96, 512], P(('clips', 'tm'), 'height'), parts along dimension 0, may hold values from -1000 to 1000
- gain: float32 [512], replicated, may hold values from 0.1 to 1.9
- shift: float32 [512], replicated, may hold values from -3 to 3
- kernel: bfloat16 [3, 3, 3, 512, 256], replicated, may hold values from -0.0546875 to 0.0546875
- bias: float32 [256], replicated, may hold values from -3 to 3
Outputs:
- decoded: bfloat16 [16, 16, 96, 256], P(('clips', 'tm'), 'height'), parts along dimension 0
There are 2 independent parts, one for each index of `clips`. A program takes and returns all parts, laid end to end along the dimension named above; an argument that names none is the same for every part. Nothing has to cross between parts.
All inputs are finite; a program needn't handle non-finite values.
Results may differ from a plain program's by a relative error of at most 0.0055.
Values may be sent and summed in bfloat16 or wider, within the bound.
No kernel may reach another device: no remote copies, remote signals or barrier semaphores. Data moves between devices by JAX's collectives and lax.ppermute only.
A program may use at most 64 MiB of HBM per device.

v0:
```python
import jax
import jax.numpy as jnp
from jax import lax
from jax.sharding import PartitionSpec as P

GROUPS = 32


epsilon = 1e-06


def passed_along(value, axis, steps):
    count = lax.axis_size(axis)
    initial, last = (max(0, -steps), min(count, count - steps))
    return lax.ppermute(value, axis, [(source, source + steps) for source in range(initial, last)])


def padded(block, sides, width):
    for axis, dim in sides:
        count = lax.axis_size(axis)
        forward = [(i, i + 1) for i in range(count - 1)]
        backward = [(target, source) for source, target in forward]
        low = lax.ppermute(
            lax.slice_in_dim(block, block.shape[dim] - width, None, axis=dim), axis, forward
        )
        high = lax.ppermute(lax.slice_in_dim(block, 0, width, axis=dim), axis, backward)
        block = jnp.concatenate([low, block, high], axis=dim)
    return block


def spatial(frames, kernel_plane):
    count_frames, padded_rows, padded_cols, channels = frames.shape
    inner_rows = padded_rows - 2
    inner_cols = padded_cols - 2
    summed = jnp.zeros(
        (count_frames * inner_rows * inner_cols, kernel_plane.shape[-1]), jnp.float32
    )
    for b in range(3):
        for c in range(3):
            window = frames[:, b : b + inner_rows, c : c + inner_cols, :].reshape(-1, channels)
            summed = summed + jnp.dot(
                window, kernel_plane[b, c], preferred_element_type=jnp.float32
            )
    return summed.reshape(count_frames, inner_rows, inner_cols, -1)


def pad_columns(frames):
    return jnp.pad(frames, ((0, 0), (0, 0), (1, 1), (0, 0)))


def on_device(features, gain, shift, kernel, bias):
    frames_dev, rows_dev, cols_dev, channels = features.shape
    per_group = channels // GROUPS
    wide_values = features.astype(jnp.float32).reshape(
        frames_dev, rows_dev, cols_dev, GROUPS, per_group
    )
    cells_total = (
        lax.axis_size("tm") * lax.axis_size("height") * frames_dev * rows_dev * cols_dev * per_group
    )
    local_sums = jnp.sum(wide_values, axis=(0, 1, 2, 4))
    squares = jnp.sum(wide_values * wide_values, axis=(0, 1, 2, 4))
    summed_all, squares_all = lax.psum((local_sums, squares), ("tm", "height"))
    group_mean = summed_all / cells_total
    group_var = squares_all / cells_total - group_mean * group_mean
    centered = wide_values - group_mean[:, None]
    normed = centered * lax.rsqrt(group_var + epsilon)[:, None]
    normed = normed.reshape(frames_dev, rows_dev, cols_dev, channels) * gain + shift
    activated = jax.nn.silu(normed).astype(jnp.bfloat16)
    tm_index = lax.axis_index("tm")
    first_pair = jnp.concatenate([activated[:1], activated[:1]], 0)
    earlier = passed_along(activated, "tm", 1)
    earlier = jnp.where(tm_index == 0, first_pair, earlier)
    slab = jnp.concatenate([earlier, activated], 0)
    slab = pad_columns(padded(slab, (("height", 1),), 1))
    output = jnp.zeros((frames_dev, rows_dev, cols_dev, kernel.shape[-1]), jnp.float32)
    for a in range(3):
        output = output + spatial(slab[a : a + frames_dev], kernel[a])
    return (output + bias).astype(jnp.bfloat16)


def solution(mesh):
    placed = (P(("clips", "tm"), "height", None, None), P(), P(), P(), P())
    return jax.shard_map(
        on_device,
        mesh=mesh,
        in_specs=placed,
        out_specs=P(("clips", "tm"), "height", None, None),
        check_vma=False,
    )
```

profile of v0, /device:TPU:4, one launch (start us, length us, event | category | flops | bytes accessed | tf_op | source)
XLA Modules:
  0.0 82.0 jit_solution(8100882752288773992)
XLA Ops:
  0.0 1.4 %convert_reduce_fusion = (f32[512]{0:T(512)S(1)}, f32[512]{0:T(512)S(1)}) fusion(bf16[2,4,96,512]{3,2,1,0:T(8,128)(2,1)} %param.5), kind=kLoop, calls=%fused_computation.10 | loop fusion | flops 1571840 | bytes 790528 | tf_op jit(solution)/shard_map/reduce_sum | solution.py:60
  1.8 32.7 %all-reduce.1 = (f32[32]{0:T(128)S(1)}, f32[32]{0:T(128)S(1)}) all-reduce(f32[32]{0:T(128)S(1)} %reduce_sum.37, f32[32]{0:T(128)S(1)} %reduce_sum.25), channel_id=1, replica_groups=mesh['clips'=2,'tm'=4,'height'=4] {'tm','height'}, use_global_device_ids=true, to_apply=%region_5.6 | all-reduce | flops 64 | bytes 512 | tf_op jit(solution)/shard_map/psum | solution.py:62
  34.8 1.7 %fusion.12 = bf16[2,4,96,512]{3,2,1,0:T(8,128)(2,1)S(1)} fusion(bf16[2,4,96,512]{3,2,1,0:T(8,128)(2,1)} %param.5, f32[512]{0:T(512)} %param.7, f32[512]{0:T(512)} %param.6, f32[512]{0:T(512)S(1)} %mul.35, f32[512]{0:T(512)S(1)} %sub.17), kind=kLoop, calls=%fused_computation.24 | loop fusion | flops 3932160 | bytes 1581056 | tf_op jit(solution)/shard_map/convert_element_type | solution.py:68
  36.5 1.9 %collective-permute-start = (bf16[2,4,96,512]{3,2,1,0:T(8,128)(2,1)S(1)}, bf16[2,4,96,512]{3,2,1,0:T(8,128)(2,1)S(1)}, u32[]{:S(2)}, u32[]{:S(2)}) collective-permute-start(bf16[2,4,96,512]{3,2,1,0:T(8,128)(2,1)S(1)} %fusion.12), channel_id=1, source_target_pairs={{0,4},{4,8},{8,12},{1,5},{5,9},{9,13},{2,6},{6,10},{10,14},{3,7},{... | collective-permute-start | bytes 2359304 | tf_op jit(solution)/shard_map/ppermute | solution.py:15
  38.5 3.8 %slice_bitcast_fusion.2 = (bf16[3,3,512,256]{3,2,1,0:T(8,128)(2,1)S(1)}, bf16[3,3,512,256]{3,2,1,0:T(8,128)(2,1)S(1)}, bf16[3,3,512,256]{3,2,1,0:T(8,128)(2,1)S(1)}) fusion(bf16[3,3,3,512,256]{4,3,2,1,0:T(8,128)(2,1)} %param.8), kind=kLoop, calls=%fused_computation.13 | loop fusion | bytes 14155776 | tf_op jit(solution)/shard_map/squeeze | solution.py:77
  42.3 0.4 fusion.24
  42.7 7.1 %collective-permute-done = bf16[2,4,96,512]{3,2,1,0:T(8,128)(2,1)S(1)} collective-permute-done((bf16[2,4,96,512]{3,2,1,0:T(8,128)(2,1)S(1)}, bf16[2,4,96,512]{3,2,1,0:T(8,128)(2,1)S(1)}, u32[]{:S(2)}, u32[]{:S(2)}) %collective-permute-start) | collective-permute-done | bytes 786464 | tf_op jit(solution)/shard_map/ppermute | solution.py:15
  50.1 1.3 %collective-permute-start.1 = (bf16[4,1,96,512]{3,2,1,0:T(8,128)(2,1)S(1)}, bf16[4,1,96,512]{3,2,1,0:T(8,128)(2,1)S(1)}, u32[]{:S(2)}, u32[]{:S(2)}) collective-permute-start(bf16[4,1,96,512]{3,2,1,0:T(8,128)(2,1)S(1)} %get-tuple-element.38), channel_id=1, source_target_pairs={{0,1},{1,2},{2,3},{4,5},{5,6},{6,7},{8,9},{9,10},{10,11},{12,13},{... | collective-permute-start | bytes 1179656 | tf_op jit(solution)/shard_map/ppermute | solution.py:23
  51.4 1.5 %collective-permute-start.2 = (bf16[4,1,96,512]{3,2,1,0:T(8,128)(2,1)S(1)}, bf16[4,1,96,512]{3,2,1,0:T(8,128)(2,1)S(1)}, u32[]{:S(2)}, u32[]{:S(2)}) collective-permute-start(bf16[4,1,96,512]{3,2,1,0:T(8,128)(2,1)S(1)} %get-tuple-element.39), channel_id=1, source_target_pairs={{1,0},{2,1},{3,2},{5,4},{6,5},{7,6},{9,8},{10,9},{11,10},{13,12},{... | collective-permute-start | bytes 1179656 | tf_op jit(solution)/shard_map/ppermute | solution.py:26
  52.9 1.3 %fusion.32 = f32[768,256]{1,0:T(8,128)} fusion(bf16[768,512]{1,0:T(8,128)(2,1)S(1)} %bitcast.169, bf16[3,3,512,256]{3,2,1,0:T(8,128)(2,1)S(1)} %get-tuple-element.11), kind=kOutput, calls=%fused_computation.65 | convolution fusion | flops 201326592 | bytes 1835008 | tf_op jit(solution)/shard_map/dot_general | solution.py:41
  54.5 2.1 %collective-permute-done.1 = bf16[4,1,96,512]{3,2,1,0:T(8,128)(2,1)S(1)} collective-permute-done((bf16[4,1,96,512]{3,2,1,0:T(8,128)(2,1)S(1)}, bf16[4,1,96,512]{3,2,1,0:T(8,128)(2,1)S(1)}, u32[]{:S(2)}, u32[]{:S(2)}) %collective-permute-start.1) | collective-permute-done | bytes 393248 | tf_op jit(solution)/shard_map/ppermute | solution.py:23
  56.6 4.4 %collective-permute-done.2 = bf16[4,1,96,512]{3,2,1,0:T(8,128)(2,1)S(1)} collective-permute-done((bf16[4,1,96,512]{3,2,1,0:T(8,128)(2,1)S(1)}, bf16[4,1,96,512]{3,2,1,0:T(8,128)(2,1)S(1)}, u32[]{:S(2)}, u32[]{:S(2)}) %collective-permute-start.2) | collective-permute-done | bytes 393248 | tf_op jit(solution)/shard_map/ppermute | solution.py:26
  61.1 0.5 maximum_maximum_fusion
  61.5 1.5 %fusion.47 = (bf16[2,4,96,512]{3,2,1,0:T(8,128)(2,1)}, bf16[2,4,96,512]{3,2,1,0:T(8,128)(2,1)}, bf16[2,4,96,512]{3,2,1,0:T(8,128)(2,1)S(1)}, bf16[2,4,96,512]{3,...) fusion(bf16[4,5,96,512]{3,2,1,0:T(8,128)(2,1)S(1)} %get-tuple-element.36, ...), kind=kLoop, calls=%fused_computation.95 | loop fusion | bytes 9437184 | tf_op jit(solution)/shard_map/slice | solution.py:40
  63.1 1.3 %fusion.30 = f32[768,256]{1,0:T(8,128)} fusion(bf16[768,512]{1,0:T(8,128)(2,1)S(1)} %bitcast.168, bf16[3,3,512,256]{3,2,1,0:T(8,128)(2,1)S(1)} %get-tuple-element.11), kind=kOutput, calls=%fused_computation.60 | convolution fusion | flops 201326592 | bytes 1835008 | tf_op jit(solution)/shard_map/dot_general | solution.py:41
  64.3 1.3 %fusion.35 = f32[768,256]{1,0:T(8,128)} fusion(bf16[768,512]{1,0:T(8,128)(2,1)S(1)} %bitcast.167, bf16[3,3,512,256]{3,2,1,0:T(8,128)(2,1)S(1)} %get-tuple-element.11), kind=kOutput, calls=%fused_computation.71 | convolution fusion | flops 201326592 | bytes 1835008 | tf_op jit(solution)/shard_map/dot_general | solution.py:41
  65.6 1.5 %select_maximum_fusion = bf16[4,6,98,512]{3,2,1,0:T(8,128)(2,1)S(1)} fusion(bf16[4,1,96,512]{3,2,1,0:T(8,128)(2,1)S(1)} %collective-permute-done.2, bf16[4,1,96,512]{3,2,1,0:T(8,128)(2,1)S(1)} %collective-permute-done.1, bf16[2,4,96,512]{3,2,1,0:T(8,128)(2,1)S(1)} %fusion.12, bf16[2,4,96,512]{3,2,1,0:T(8,128)(2,1)S(1)} %maximum_select_fusion), kind=kLoop, calls=%fused_computation.3 | loop fusion | flops 18063360 | bytes 4767744 | tf_op jit(solution)/shard_map/concatenate | solution.py:27
  67.1 4.6 %fusion.46 = (bf16[2,4,96,512]{3,2,1,0:T(8,128)(2,1)S(1)}, bf16[2,4,96,512]{3,2,1,0:T(8,128)(2,1)S(1)}, bf16[2,4,96,512]{3,2,1,0:T(8,128)(2,1)S(1)}, bf16[2,4,96...) fusion(bf16[4,6,98,512]{3,2,1,0:T(8,128)(2,1)S(1)} %select_maxi, ...), kind=kLoop, calls=%fused_computation.94 | loop fusion | bytes 28311552 | tf_op jit(solution)/shard_map/slice | solution.py:40
  74.5 0.4 fusion.27
  76.0 0.4 fusion.25
  77.1 0.4 fusion.37
  79.8 0.4 fusion.20
  80.3 0.9 %fusion.17 = f32[768,256]{1,0:T(8,128)S(1)} fusion(f32[768,256]{1,0:T(8,128)S(1)} %fusion.21, f32[768,256]{1,0:T(8,128)S(1)} %fusion.22, f32[768,256]{1,0:T(8,128)S(1)} %fusion.23, bf16[768,512]{1,0:T(8,128)(2,1)S(1)} %bitcast.144, f32[768,256]{1,0:T(8,128)S(1)} %fusion.24, f32[768,256]{1,0:T(8,128)S(1)} %fusion.25, f32[768,256]{1,0:T(8,128)S(1)} %fusion.26, ...), kind=kOutput, calls=%fused_computation.30 | convolution fusion | flops 204865536 | bytes 15990784 | tf_op jit(solution)/shard_map/dot_general | solution.py:41
  81.2 0.8 add_convert_fusion
  (45 shorter events, 8.1 us)
Async XLA Ops:
  36.5 13.3 %collective-permute-start = (bf16[2,4,96,512]{3,2,1,0:T(8,128)(2,1)S(1)}, bf16[2,4,96,512]{3,2,1,0:T(8,128)(2,1)S(1)}, u32[]{:S(2)}, u32[]{:S(2)}) collective-permute-start(bf16[2,4,96,512]{3,2,1,0:T(8,128)(2,1)S(1)} %fusion.12), channel_id=1, source_target_pairs={{0,4},{4,8},{8,12},{1,5},{5,9},{9,13},{2,6},{6,10},{10,14},{3,7},{... | collective-permute-start | bytes 2359304 | tf_op jit(solution)/shard_map/ppermute | solution.py:15
  50.1 6.6 %collective-permute-start.1 = (bf16[4,1,96,512]{3,2,1,0:T(8,128)(2,1)S(1)}, bf16[4,1,96,512]{3,2,1,0:T(8,128)(2,1)S(1)}, u32[]{:S(2)}, u32[]{:S(2)}) collective-permute-start(bf16[4,1,96,512]{3,2,1,0:T(8,128)(2,1)S(1)} %get-tuple-element.38), channel_id=1, source_target_pairs={{0,1},{1,2},{2,3},{4,5},{5,6},{6,7},{8,9},{9,10},{10,11},{12,13},{... | collective-permute-start | bytes 1179656 | tf_op jit(solution)/shard_map/ppermute | solution.py:23
  51.4 9.7 %collective-permute-start.2 = (bf16[4,1,96,512]{3,2,1,0:T(8,128)(2,1)S(1)}, bf16[4,1,96,512]{3,2,1,0:T(8,128)(2,1)S(1)}, u32[]{:S(2)}, u32[]{:S(2)}) collective-permute-start(bf16[4,1,96,512]{3,2,1,0:T(8,128)(2,1)S(1)} %get-tuple-element.39), channel_id=1, source_target_pairs={{1,0},{2,1},{3,2},{5,4},{6,5},{7,6},{9,8},{10,9},{11,10},{13,12},{... | collective-permute-start | bytes 1179656 | tf_op jit(solution)/shard_map/ppermute | solution.py:26
  72.5 1.1 %copy-start.2 = (bf16[2,4,96,512]{3,2,1,0:T(8,128)(2,1)S(1)}, bf16[2,4,96,512]{3,2,1,0:T(8,128)(2,1)}, u32[]{:S(2)}) copy-start(bf16[2,4,96,512]{3,2,1,0:T(8,128)(2,1)} %get-tuple-element.44) | copy-start | bytes 2359300
  72.9 1.2 %copy-start.1 = (bf16[2,4,96,512]{3,2,1,0:T(8,128)(2,1)S(1)}, bf16[2,4,96,512]{3,2,1,0:T(8,128)(2,1)}, u32[]{:S(2)}) copy-start(bf16[2,4,96,512]{3,2,1,0:T(8,128)(2,1)} %get-tuple-element.30) | copy-start | bytes 2359300
  73.2 1.3 %copy-start = (bf16[2,4,96,512]{3,2,1,0:T(8,128)(2,1)S(1)}, bf16[2,4,96,512]{3,2,1,0:T(8,128)(2,1)}, u32[]{:S(2)}) copy-start(bf16[2,4,96,512]{3,2,1,0:T(8,128)(2,1)} %get-tuple-element.31) | copy-start | bytes 2359300
  78.2 1.1 %copy-start.3 = (f32[768,256]{1,0:T(8,128)S(1)}, f32[768,256]{1,0:T(8,128)}, u32[]{:S(2)}) copy-start(f32[768,256]{1,0:T(8,128)} %fusion.32) | copy-start | bytes 2359300
  78.2 1.4 %copy-start.4 = (f32[768,256]{1,0:T(8,128)S(1)}, f32[768,256]{1,0:T(8,128)}, u32[]{:S(2)}) copy-start(f32[768,256]{1,0:T(8,128)} %fusion.30) | copy-start | bytes 2359300
  78.2 1.6 %copy-start.5 = (f32[768,256]{1,0:T(8,128)S(1)}, f32[768,256]{1,0:T(8,128)}, u32[]{:S(2)}) copy-start(f32[768,256]{1,0:T(8,128)} %fusion.35) | copy-start | bytes 2359300
  80.3 0.9 %copy-start.6 = (f32[256]{0:T(256)S(1)}, f32[256]{0:T(256)}, u32[]{:S(2)}) copy-start(f32[256]{0:T(256)} %param.9) | copy-start | bytes 3076
where the time goes:
time: 82.3 us; the launch traced here: 82 us
  blocking collectives  32.7 us (40%)
  waiting for transfers between devices  13.7 us (17%)
  matrix products  13.1 us (16%)
  local copies, waits for them, and re-layouts  11.1 us (13%)
  other arithmetic  6.37 us (8%)
  starting transfers between devices  4.71 us (6%)
    psum x1, blocking collectives, on_device(): summed_all, squares_all = lax.psum((local_sums, squares), ('tm', 'height'))  32.7 us
    dot_general x27, matrix products, spatial(): jnp.dot(window, kernel_plane[b, c], preferred_element_type=jnp.float32)  13.1 us
    ppermute x1, waiting for transfers between devices, passed_along(): lax.ppermute(value, axis, [(source, source + steps) for source in range(i...  7.11 us
    slice x2, local copies, waits for them, and re-layouts, spatial(): frames[:, b:b + inner_rows, c:c + inner_cols, :].reshape(-1, channels)  6.15 us
    ppermute x1, waiting for transfers between devices, padded(): lax.ppermute(lax.slice_in_dim(block, 0, width, axis=dim), axis, backward)  4.42 us
    squeeze x1, local copies, waits for them, and re-layouts, on_device(): output = output + spatial(slab[a:a + frames_dev], kernel[a])  3.84 us
    ppermute x1, waiting for transfers between devices, padded(): lax.ppermute(lax.slice_in_dim(block, block.shape[dim] - width, None, axis...  2.14 us
    concatenate x2, other arithmetic, padded(): block = jnp.concatenate([low, block, high], axis=dim)  1.97 us
  transfers between devices with their start and end apart: 3, of which 3 were waited for; matrix products, arithmetic and copies ran while one was open for 7% of the time, Pallas kernels for 0%

commit v1 on v0

v1 whole, which is shorter than its diff:
```python
import functools

import jax
import jax.numpy as jnp
from jax import lax
from jax.experimental import pallas as pl
from jax.experimental.pallas import tpu as pltpu
from jax.sharding import PartitionSpec as P

GROUPS = 32
LANES = 128
epsilon = 1e-06
both = ("tm", "height")


def stats_kernel(x_ref, out_ref):
    frames, rows, cols, channels = x_ref.shape
    tiles = channels // LANES
    total = jnp.zeros((8, channels), jnp.float32)
    squares = jnp.zeros((8, channels), jnp.float32)
    for f in range(frames):
        for r in range(rows):
            wide = x_ref[f, r].astype(jnp.float32).reshape(cols // 8, 8, channels)
            total = total + jnp.sum(wide, axis=0)
            squares = squares + jnp.sum(wide * wide, axis=0)
    total = jnp.sum(total, axis=0, keepdims=True)
    squares = jnp.sum(squares, axis=0, keepdims=True)
    for i in range(tiles):
        out_ref[i : i + 1, :] = total[:, i * LANES : (i + 1) * LANES]
        out_ref[tiles + i : tiles + i + 1, :] = squares[:, i * LANES : (i + 1) * LANES]


def local_stats(features):
    channels = features.shape[-1]
    return pl.pallas_call(
        stats_kernel,
        out_shape=jax.ShapeDtypeStruct((2 * channels // LANES, LANES), jnp.float32),
        name="stats",
    )(features)


def summed_over(value, axis):
    count = lax.axis_size(axis)
    if count & (count - 1):
        return lax.psum(value, axis)
    step = count // 2
    while step:
        value = value + lax.ppermute(value, axis, [(i, i ^ step) for i in range(count)])
        step //= 2
    return value


def moved(value, tm_step, height_step):
    tm, height = lax.axis_size("tm"), lax.axis_size("height")
    pairs = [
        (t * height + h, (t + tm_step) * height + h + height_step)
        for t in range(tm)
        for h in range(height)
        if 0 <= t + tm_step < tm and 0 <= h + height_step < height
    ]
    return lax.ppermute(value, both, pairs)


def conv_kernel(
    cells,
    sums_ref,
    gain_ref,
    shift_ref,
    bias_ref,
    own_ref,
    earlier_ref,
    above_ref,
    below_ref,
    early_above_ref,
    early_below_ref,
    kernel_ref,
    out_ref,
    raw,
    act,
    weights,
    acc,
    coef,
    slab_sem,
    weight_sem,
):
    frames, rows, cols, channels = own_ref.shape
    tiles = channels // LANES
    cout = out_ref.shape[-1]
    tm = lax.axis_index("tm")
    height = lax.axis_index("height")
    last = lax.axis_size("height") - 1

    def copies(first):
        early = [own_ref.at[0:1]] * 2 if first else [earlier_ref.at[0:1], earlier_ref.at[1:2]]
        early_above = [above_ref.at[0:1]] * 2 if first else [early_above_ref.at[0:1], early_above_ref.at[1:2]]
        early_below = [below_ref.at[0:1]] * 2 if first else [early_below_ref.at[0:1], early_below_ref.at[1:2]]
        n = 0
        out = []
        for i in range(2):
            for source, start, size in (
                (early[i], 1, rows),
                (early_above[i], 0, 1),
                (early_below[i], rows + 1, 1),
            ):
                out.append(
                    pltpu.make_async_copy(
                        source, raw.at[i : i + 1, start : start + size], slab_sem.at[3 + n]
                    )
                )
                n += 1
        return out

    own_copies = [
        pltpu.make_async_copy(own_ref, raw.at[2 : 2 + frames, 1 : 1 + rows], slab_sem.at[0]),
        pltpu.make_async_copy(above_ref, raw.at[2 : 2 + frames, 0:1], slab_sem.at[1]),
        pltpu.make_async_copy(below_ref, raw.at[2 : 2 + frames, rows + 1 : rows + 2], slab_sem.at[2]),
    ]
    for copy in own_copies:
        copy.start()

    @pl.when(tm == 0)
    def _():
        for copy in copies(True):
            copy.start()

    @pl.when(tm != 0)
    def _():
        for copy in copies(False):
            copy.start()

    weight_copies = [
        pltpu.make_async_copy(kernel_ref.at[a], weights.at[a], weight_sem.at[a]) for a in range(3)
    ]
    for copy in weight_copies:
        copy.start()

    per_group = channels // GROUPS
    row = lax.broadcasted_iota(jnp.int32, (LANES, LANES), 0) // per_group
    col = lax.broadcasted_iota(jnp.int32, (LANES, LANES), 1) // per_group
    same = jnp.where(row == col, 1.0, 0.0)
    grouped = jnp.dot(
        sums_ref[...], same, precision=lax.Precision.HIGHEST, preferred_element_type=jnp.float32
    )
    mean = grouped[:tiles] / cells
    var = grouped[tiles:] / cells - mean * mean
    scale = lax.rsqrt(var + epsilon) * gain_ref[...]
    offset = shift_ref[...] - mean * scale
    for i in range(tiles):
        coef[0:1, i * LANES : (i + 1) * LANES] = 0.5 * scale[i : i + 1]
        coef[1:2, i * LANES : (i + 1) * LANES] = 0.5 * offset[i : i + 1]

    for copy in own_copies:
        copy.wait()
    for copy in copies(False):
        copy.wait()

    half_scale = coef[0:1, :]
    half_offset = coef[1:2, :]
    top = jnp.where(height == 0, 0.0, 1.0)
    bottom = jnp.where(height == last, 0.0, 1.0)

    for f in range(2 + frames):
        for r in range(rows + 2):
            half = raw[f, r].astype(jnp.float32) * half_scale + half_offset
            value = half + half * jnp.tanh(half)
            if r == 0:
                value = value * top
            if r == rows + 1:
                value = value * bottom
            act[f, r] = value.astype(jnp.bfloat16)

    for copy in weight_copies:
        copy.wait()

    for c in range(3):
        total = None
        for a in range(3):
            windows = [
                act[a : a + frames, b : b + rows].reshape(frames * rows * cols, channels)
                for b in range(3)
            ]
            part = jnp.dot(
                jnp.concatenate(windows, axis=1),
                weights[a, :, c].reshape(3 * channels, cout),
                preferred_element_type=jnp.float32,
            )
            total = part if total is None else total + part
        acc[c] = total.reshape(frames * rows, cols, cout)

    place = lax.broadcasted_iota(jnp.int32, (cols, cout), 0)
    for i in range(frames * rows):
        left = jnp.where(place == 0, 0.0, pltpu.roll(acc[0, i], 1, 0))
        right = jnp.where(place == cols - 1, 0.0, pltpu.roll(acc[2, i], cols - 1, 0))
        out_ref[i // rows, i % rows] = (acc[1, i] + left + right + bias_ref[...]).astype(jnp.bfloat16)


def on_device(features, gain, shift, kernel, bias):
    frames, rows, cols, channels = features.shape
    cout = kernel.shape[-1]
    tiles = channels // LANES
    cells = lax.axis_size("tm") * lax.axis_size("height") * frames * rows * cols * (channels // GROUPS)
    first_row, last_row = features[:, :1], features[:, rows - 1 :]
    sums = local_stats(features)
    sums = summed_over(summed_over(sums, "tm"), "height")
    earlier = moved(features, 1, 0)
    above = moved(last_row, 0, 1)
    below = moved(first_row, 0, -1)
    early_above = moved(last_row, 1, 1)
    early_below = moved(first_row, 1, -1)
    vmem = pl.BlockSpec(memory_space=pltpu.VMEM)
    hbm = pl.BlockSpec(memory_space=pl.ANY)
    return pl.pallas_call(
        functools.partial(conv_kernel, float(cells)),
        out_shape=jax.ShapeDtypeStruct((frames, rows, cols, cout), jnp.bfloat16),
        in_specs=[vmem] * 4 + [hbm] * 7,
        out_specs=vmem,
        scratch_shapes=[
            pltpu.VMEM((2 + frames, rows + 2, cols, channels), jnp.bfloat16),
            pltpu.VMEM((2 + frames, rows + 2, cols, channels), jnp.bfloat16),
            pltpu.VMEM(kernel.shape, jnp.bfloat16),
            pltpu.VMEM((3, frames * rows, cols, cout), jnp.float32),
            pltpu.VMEM((8, channels), jnp.float32),
            pltpu.SemaphoreType.DMA((9,)),
            pltpu.SemaphoreType.DMA((3,)),
        ],
        compiler_params=pltpu.CompilerParams(vmem_limit_bytes=48 * 1024 * 1024),
        name="conv",
    )(
        sums,
        gain.reshape(tiles, LANES),
        shift.reshape(tiles, LANES),
        bias.reshape(1, cout),
        features,
        earlier,
        above,
        below,
        early_above,
        early_below,
        kernel,
    )


def solution(mesh):
    placed = (P(("clips", "tm"), "height", None, None), P(), P(), P(), P())
    return jax.shard_map(
        on_device,
        mesh=mesh,
        in_specs=placed,
        out_specs=P(("clips", "tm"), "height", None, None),
        check_vma=False,
    )
```

time: 82.3 us -> 55.2 us (0.67)
  the two profiles are of different devices: /device:TPU:4 before, /device:TPU:0 now
where the time goes in v1:
time: 55.2 us; the launch traced here: 54.8 us
  starting transfers between devices  27.7 us (50%)
  Pallas kernels  12.7 us (23%)
  waiting for transfers between devices  9.4 us (17%)
  local copies, waits for them, and re-layouts  4.22 us (8%)
  other arithmetic  0.7 us (1%)
    ppermute x5, starting transfers between devices, moved(): return lax.ppermute(value, both, pairs)  15.4 us
    ppermute x4, starting transfers between devices, summed_over(): lax.ppermute(value, axis, [(i, i ^ step) for i in range(count)])  12.3 us
    pallas_call x1, Pallas kernels, on_device(): pl.pallas_call(functools.partial(conv_kernel, float(cells)), out_shape=ja...  10.8 us
    ppermute x5, waiting for transfers between devices, moved(): return lax.ppermute(value, both, pairs)  4.86 us
    ppermute x4, waiting for transfers between devices, summed_over(): lax.ppermute(value, axis, [(i, i ^ step) for i in range(count)])  4.54 us
    unnamed x8, local copies, waits for them, and re-layouts  3.17 us
    pallas_call x1, Pallas kernels, local_stats(): pl.pallas_call(stats_kernel, out_shape=jax.ShapeDtypeStruct((2 * channels...  1.88 us
  transfers between devices with their start and end apart: 9, of which 5 were waited for; matrix products, arithmetic and copies ran while one was open for 3% of the time, Pallas kernels for 3%

profile of v1, /device:TPU:0, one launch (start us, length us, event | category | flops | bytes accessed | tf_op | source)
XLA Modules:
  0.0 54.8 jit_solution(4717742011338999860)
XLA Ops:
  0.0 2.4 %collective-permute-start.4 = (bf16[2,4,96,512]{3,2,1,0:T(8,128)(2,1)}, bf16[2,4,96,512]{3,2,1,0:T(8,128)(2,1)S(1)}, u32[]{:S(2)}, u32[]{:S(2)}) collective-permute-start(bf16[2,4,96,512]{3,2,1,0:T(8,128)(2,1)} %own_ref.1), channel_id=1, source_target_pairs={{0,4},{1,5},{2,6},{3,7},{4,8},{5,9},{6,10},{7,11},{8,12},{9,13},{1... | collective-permute-start | bytes 2359304 | tf_op jit(solution)/shard_map/ppermute | solution.py:61
  2.4 1.9 %stats.1 = f32[8,128]{1,0:T(8,128)} custom-call(bf16[2,4,96,512]{3,2,1,0:T(8,128)(2,1)} %own_ref.1), custom_call_target="tpu_custom_call" | custom-call | tf_op jit(solution)/shard_map/stats/pallas_call | solution.py:35
  4.3 2.5 %collective-permute-start = (f32[8,128]{1,0:T(8,128)}, f32[8,128]{1,0:T(8,128)S(1)}, u32[]{:S(2)}, u32[]{:S(2)}) collective-permute-start(f32[8,128]{1,0:T(8,128)} %stats.1), channel_id=1, source_target_pairs={{0,8},{4,12},{8,0},{12,4},{1,9},{5,13},{9,1},{13,5},{2,10},{6,14},... | collective-permute-start | bytes 12296 | tf_op jit(solution)/shard_map/ppermute | solution.py:48
  6.8 1.8 %collective-permute-done = f32[8,128]{1,0:T(8,128)S(1)} collective-permute-done((f32[8,128]{1,0:T(8,128)}, f32[8,128]{1,0:T(8,128)S(1)}, u32[]{:S(2)}, u32[]{:S(2)}) %collective-permute-start) | collective-permute-done | bytes 4128 | tf_op jit(solution)/shard_map/ppermute | solution.py:48
  8.6 0.7 %add.12 = f32[8,128]{1,0:T(8,128)S(1)} add(f32[8,128]{1,0:T(8,128)} %stats.1, f32[8,128]{1,0:T(8,128)S(1)} %collective-permute-done) | non-fusion elementwise | flops 1024 | bytes 12288 | tf_op jit(solution)/shard_map/add | solution.py:48
  9.3 5.7 %collective-permute-start.1 = (f32[8,128]{1,0:T(8,128)S(1)}, f32[8,128]{1,0:T(8,128)S(1)}, u32[]{:S(2)}, u32[]{:S(2)}) collective-permute-start(f32[8,128]{1,0:T(8,128)S(1)} %add.12), channel_id=1, source_target_pairs={{0,4},{4,0},{8,12},{12,8},{1,5},{5,1},{9,13},{13,9},{2,6},{6,2},{1... | collective-permute-start | bytes 12296 | tf_op jit(solution)/shard_map/ppermute | solution.py:48
  15.0 0.8 %collective-permute-done.1 = f32[8,128]{1,0:T(8,128)S(1)} collective-permute-done((f32[8,128]{1,0:T(8,128)S(1)}, f32[8,128]{1,0:T(8,128)S(1)}, u32[]{:S(2)}, u32[]{:S(2)}) %collective-permute-start.1) | collective-permute-done | bytes 4128 | tf_op jit(solution)/shard_map/ppermute | solution.py:48
  15.8 2.6 %collective-permute-start.2 = (f32[8,128]{1,0:T(8,128)S(1)}, f32[8,128]{1,0:T(8,128)S(1)}, u32[]{:S(2)}, u32[]{:S(2)}) collective-permute-start(f32[8,128]{1,0:T(8,128)S(1)} %add.13), channel_id=1, source_target_pairs={{0,2},{1,3},{2,0},{3,1},{4,6},{5,7},{6,4},{7,5},{8,10},{9,11},{10,... | collective-permute-start | bytes 12296 | tf_op jit(solution)/shard_map/ppermute | solution.py:48
  18.4 1.9 %collective-permute-done.2 = f32[8,128]{1,0:T(8,128)S(1)} collective-permute-done((f32[8,128]{1,0:T(8,128)S(1)}, f32[8,128]{1,0:T(8,128)S(1)}, u32[]{:S(2)}, u32[]{:S(2)}) %collective-permute-start.2) | collective-permute-done | bytes 4128 | tf_op jit(solution)/shard_map/ppermute | solution.py:48
  20.3 1.6 %collective-permute-start.3 = (f32[8,128]{1,0:T(8,128)S(1)}, f32[8,128]{1,0:T(8,128)S(1)}, u32[]{:S(2)}, u32[]{:S(2)}) collective-permute-start(f32[8,128]{1,0:T(8,128)S(1)} %add.14), channel_id=1, source_target_pairs={{0,1},{1,0},{2,3},{3,2},{4,5},{5,4},{6,7},{7,6},{8,9},{9,8},{10,11... | collective-permute-start | bytes 12296 | tf_op jit(solution)/shard_map/ppermute | solution.py:48
  21.9 1.0 %fusion = (bf16[2,1,96,512]{3,2,1,0:T(8,128)(2,1)S(1)}, bf16[2,1,96,512]{3,2,1,0:T(8,128)(2,1)S(1)}) fusion(bf16[2,4,96,512]{3,2,1,0:T(8,128)(2,1)} %own_ref.1), kind=kLoop, calls=%fused_computation | loop fusion | bytes 786432 | tf_op jit(solution)/shard_map/slice | solution.py:202
  22.9 0.7 %collective-permute-start.8 = (bf16[2,1,96,512]{3,2,1,0:T(8,128)(2,1)S(1)}, bf16[2,1,96,512]{3,2,1,0:T(8,128)(2,1)S(1)}, u32[]{:S(2)}, u32[]{:S(2)}) collective-permute-start(bf16[2,1,96,512]{3,2,1,0:T(8,128)(2,1)S(1)} %get-tuple-element.5), channel_id=1, source_target_pairs={{1,4},{2,5},{3,6},{5,8},{6,9},{7,10},{9,12},{10,13},{11,14},{17,20... | collective-permute-start | bytes 589832 | tf_op jit(solution)/shard_map/ppermute | solution.py:61
  23.6 1.3 %collective-permute-start.6 = (bf16[2,1,96,512]{3,2,1,0:T(8,128)(2,1)S(1)}, bf16[2,1,96,512]{3,2,1,0:T(8,128)(2,1)S(1)}, u32[]{:S(2)}, u32[]{:S(2)}) collective-permute-start(bf16[2,1,96,512]{3,2,1,0:T(8,128)(2,1)S(1)} %get-tuple-element.5), channel_id=1, source_target_pairs={{1,0},{2,1},{3,2},{5,4},{6,5},{7,6},{9,8},{10,9},{11,10},{13,12},{... | collective-permute-start | bytes 589832 | tf_op jit(solution)/shard_map/ppermute | solution.py:61
  24.9 7.3 %collective-permute-start.7 = (bf16[2,1,96,512]{3,2,1,0:T(8,128)(2,1)S(1)}, bf16[2,1,96,512]{3,2,1,0:T(8,128)(2,1)S(1)}, u32[]{:S(2)}, u32[]{:S(2)}) collective-permute-start(bf16[2,1,96,512]{3,2,1,0:T(8,128)(2,1)S(1)} %get-tuple-element.6), channel_id=1, source_target_pairs={{0,5},{1,6},{2,7},{4,9},{5,10},{6,11},{8,13},{9,14},{10,15},{16,21... | collective-permute-start | bytes 589832 | tf_op jit(solution)/shard_map/ppermute | solution.py:61
  32.3 3.6 %collective-permute-start.5 = (bf16[2,1,96,512]{3,2,1,0:T(8,128)(2,1)S(1)}, bf16[2,1,96,512]{3,2,1,0:T(8,128)(2,1)S(1)}, u32[]{:S(2)}, u32[]{:S(2)}) collective-permute-start(bf16[2,1,96,512]{3,2,1,0:T(8,128)(2,1)S(1)} %get-tuple-element.6), channel_id=1, source_target_pairs={{0,1},{1,2},{2,3},{4,5},{5,6},{6,7},{8,9},{9,10},{10,11},{12,13},{... | collective-permute-start | bytes 589832 | tf_op jit(solution)/shard_map/ppermute | solution.py:61
  36.0 0.0 collective-permute-done.6.below_ref
  36.0 1.4 %collective-permute-done.7.early_above_ref = bf16[2,1,96,512]{3,2,1,0:T(8,128)(2,1)S(1)} collective-permute-done((bf16[2,1,96,512]{3,2,1,0:T(8,128)(2,1)S(1)}, bf16[2,1,96,512]{3,2,1,0:T(8,128)(2,1)S(1)}, u32[]{:S(2)}, u32[]{:S(2)}) %collective-permute-start.7) | collective-permute-done | bytes 196640 | tf_op jit(solution)/shard_map/ppermute | solution.py:61
  37.4 3.4 %collective-permute-done.5.above_ref = bf16[2,1,96,512]{3,2,1,0:T(8,128)(2,1)S(1)} collective-permute-done((bf16[2,1,96,512]{3,2,1,0:T(8,128)(2,1)S(1)}, bf16[2,1,96,512]{3,2,1,0:T(8,128)(2,1)S(1)}, u32[]{:S(2)}, u32[]{:S(2)}) %collective-permute-start.5) | collective-permute-done | bytes 196640 | tf_op jit(solution)/shard_map/ppermute | solution.py:61
  40.8 0.0 collective-permute-done.4.earlier_ref
  40.8 1.1 %copy-done = bf16[2,4,96,512]{3,2,1,0:T(8,128)(2,1)S(1)} copy-done((bf16[2,4,96,512]{3,2,1,0:T(8,128)(2,1)S(1)}, bf16[2,4,96,512]{3,2,1,0:T(8,128)(2,1)}, u32[]{:S(2)}) %copy-start) | copy-done | bytes 786456
  42.0 0.7 %copy-done.1 = f32[512]{0:T(512)S(1)} copy-done((f32[512]{0:T(512)S(1)}, f32[512]{0:T(512)}, u32[]{:S(2)}) %copy-start.1) | copy-done | bytes 2072
  42.6 0.7 %copy-done.2 = f32[512]{0:T(512)S(1)} copy-done((f32[512]{0:T(512)S(1)}, f32[512]{0:T(512)}, u32[]{:S(2)}) %copy-start.2) | copy-done | bytes 2072
  43.3 0.7 %copy-done.3 = f32[256]{0:T(256)S(1)} copy-done((f32[256]{0:T(256)S(1)}, f32[256]{0:T(256)}, u32[]{:S(2)}) %copy-start.3) | copy-done | bytes 1048
  44.0 10.8 %conv.1 = bf16[2,4,96,256]{3,2,1,0:T(8,128)(2,1)} custom-call(f32[8,128]{1,0:T(8,128)S(1)} %add.15.sums_ref, f32[4,128]{1,0:T(4,128)S(1)} %bitcast.3, f32[4,128]{1,0:T(4,128)S(1)} %bitcast.4, f32[1,256]{1,0:T(1,128)S(1)} %bitcast.5, bf16[2,4,96,512]{3,2,1,0:T(8,128)(2,1)S(1)} %copy-done, bf16[2,4,96,512]{3,2,1,0:T(8,128)(2,1)S(1)} %collective-permute-done.4.earlier_ref, ...), custom_call_target="tpu_custom_call" | custom-call | tf_op jit(solution)/shard_map/conv/pallas_call | solution.py:212
  (9 shorter events, 0.0 us)
Async XLA Ops:
  0.0 40.8 %collective-permute-start.4 = (bf16[2,4,96,512]{3,2,1,0:T(8,128)(2,1)}, bf16[2,4,96,512]{3,2,1,0:T(8,128)(2,1)S(1)}, u32[]{:S(2)}, u32[]{:S(2)}) collective-permute-start(bf16[2,4,96,512]{3,2,1,0:T(8,128)(2,1)} %own_ref.1), channel_id=1, source_target_pairs={{0,4},{1,5},{2,6},{3,7},{4,8},{5,9},{6,10},{7,11},{8,12},{9,13},{1... | collective-permute-start | bytes 2359304 | tf_op jit(solution)/shard_map/ppermute | solution.py:61
  4.3 4.3 %collective-permute-start = (f32[8,128]{1,0:T(8,128)}, f32[8,128]{1,0:T(8,128)S(1)}, u32[]{:S(2)}, u32[]{:S(2)}) collective-permute-start(f32[8,128]{1,0:T(8,128)} %stats.1), channel_id=1, source_target_pairs={{0,8},{4,12},{8,0},{12,4},{1,9},{5,13},{9,1},{13,5},{2,10},{6,14},... | collective-permute-start | bytes 12296 | tf_op jit(solution)/shard_map/ppermute | solution.py:48
  9.3 6.5 %collective-permute-start.1 = (f32[8,128]{1,0:T(8,128)S(1)}, f32[8,128]{1,0:T(8,128)S(1)}, u32[]{:S(2)}, u32[]{:S(2)}) collective-permute-start(f32[8,128]{1,0:T(8,128)S(1)} %add.12), channel_id=1, source_target_pairs={{0,4},{4,0},{8,12},{12,8},{1,5},{5,1},{9,13},{13,9},{2,6},{6,2},{1... | collective-permute-start | bytes 12296 | tf_op jit(solution)/shard_map/ppermute | solution.py:48
  15.8 4.5 %collective-permute-start.2 = (f32[8,128]{1,0:T(8,128)S(1)}, f32[8,128]{1,0:T(8,128)S(1)}, u32[]{:S(2)}, u32[]{:S(2)}) collective-permute-start(f32[8,128]{1,0:T(8,128)S(1)} %add.13), channel_id=1, source_target_pairs={{0,2},{1,3},{2,0},{3,1},{4,6},{5,7},{6,4},{7,5},{8,10},{9,11},{10,... | collective-permute-start | bytes 12296 | tf_op jit(solution)/shard_map/ppermute | solution.py:48
  20.3 12.0 %collective-permute-start.3 = (f32[8,128]{1,0:T(8,128)S(1)}, f32[8,128]{1,0:T(8,128)S(1)}, u32[]{:S(2)}, u32[]{:S(2)}) collective-permute-start(f32[8,128]{1,0:T(8,128)S(1)} %add.14), channel_id=1, source_target_pairs={{0,1},{1,0},{2,3},{3,2},{4,5},{5,4},{6,7},{7,6},{8,9},{9,8},{10,11... | collective-permute-start | bytes 12296 | tf_op jit(solution)/shard_map/ppermute | solution.py:48
  22.9 13.0 %collective-permute-start.8 = (bf16[2,1,96,512]{3,2,1,0:T(8,128)(2,1)S(1)}, bf16[2,1,96,512]{3,2,1,0:T(8,128)(2,1)S(1)}, u32[]{:S(2)}, u32[]{:S(2)}) collective-permute-start(bf16[2,1,96,512]{3,2,1,0:T(8,128)(2,1)S(1)} %get-tuple-element.5), channel_id=1, source_target_pairs={{1,4},{2,5},{3,6},{5,8},{6,9},{7,10},{9,12},{10,13},{11,14},{17,20... | collective-permute-start | bytes 589832 | tf_op jit(solution)/shard_map/ppermute | solution.py:61
  23.6 12.3 %collective-permute-start.6 = (bf16[2,1,96,512]{3,2,1,0:T(8,128)(2,1)S(1)}, bf16[2,1,96,512]{3,2,1,0:T(8,128)(2,1)S(1)}, u32[]{:S(2)}, u32[]{:S(2)}) collective-permute-start(bf16[2,1,96,512]{3,2,1,0:T(8,128)(2,1)S(1)} %get-tuple-element.5), channel_id=1, source_target_pairs={{1,0},{2,1},{3,2},{5,4},{6,5},{7,6},{9,8},{10,9},{11,10},{13,12},{... | collective-permute-start | bytes 589832 | tf_op jit(solution)/shard_map/ppermute | solution.py:61
  24.9 12.5 %collective-permute-start.7 = (bf16[2,1,96,512]{3,2,1,0:T(8,128)(2,1)S(1)}, bf16[2,1,96,512]{3,2,1,0:T(8,128)(2,1)S(1)}, u32[]{:S(2)}, u32[]{:S(2)}) collective-permute-start(bf16[2,1,96,512]{3,2,1,0:T(8,128)(2,1)S(1)} %get-tuple-element.6), channel_id=1, source_target_pairs={{0,5},{1,6},{2,7},{4,9},{5,10},{6,11},{8,13},{9,14},{10,15},{16,21... | collective-permute-start | bytes 589832 | tf_op jit(solution)/shard_map/ppermute | solution.py:61
  32.3 8.5 %collective-permute-start.5 = (bf16[2,1,96,512]{3,2,1,0:T(8,128)(2,1)S(1)}, bf16[2,1,96,512]{3,2,1,0:T(8,128)(2,1)S(1)}, u32[]{:S(2)}, u32[]{:S(2)}) collective-permute-start(bf16[2,1,96,512]{3,2,1,0:T(8,128)(2,1)S(1)} %get-tuple-element.6), channel_id=1, source_target_pairs={{0,1},{1,2},{2,3},{4,5},{5,6},{6,7},{8,9},{9,10},{10,11},{12,13},{... | collective-permute-start | bytes 589832 | tf_op jit(solution)/shard_map/ppermute | solution.py:61
  40.8 1.1 %copy-start = (bf16[2,4,96,512]{3,2,1,0:T(8,128)(2,1)S(1)}, bf16[2,4,96,512]{3,2,1,0:T(8,128)(2,1)}, u32[]{:S(2)}) copy-start(bf16[2,4,96,512]{3,2,1,0:T(8,128)(2,1)} %own_ref.1) | copy-start | bytes 2359300
  42.0 0.7 %copy-start.1 = (f32[512]{0:T(512)S(1)}, f32[512]{0:T(512)}, u32[]{:S(2)}) copy-start(f32[512]{0:T(512)} %param.6) | copy-start | bytes 6148
  42.6 0.7 %copy-start.2 = (f32[512]{0:T(512)S(1)}, f32[512]{0:T(512)}, u32[]{:S(2)}) copy-start(f32[512]{0:T(512)} %param.7) | copy-start | bytes 6148
  43.3 0.7 %copy-start.3 = (f32[256]{0:T(256)S(1)}, f32[256]{0:T(256)}, u32[]{:S(2)}) copy-start(f32[256]{0:T(256)} %param.9) | copy-start | bytes 3076

commit v2 on v1

v2 whole, which is shorter than its diff:
```python
import functools

import jax
import jax.numpy as jnp
from jax import lax
from jax.experimental import pallas as pl
from jax.experimental.pallas import tpu as pltpu
from jax.sharding import PartitionSpec as P


GROUPS = 32
LANES = 128
epsilon = 1e-06
both = ("tm", "height")


def stats_kernel(x_ref, sums_ref, edges_ref, held, sem):
    frames, rows, cols, channels = x_ref.shape
    tiles = channels // LANES
    copies = [
        pltpu.make_async_copy(x_ref.at[f, r], held.at[f, r], sem.at[f * rows + r])
        for f in range(frames)
        for r in range(rows)
    ]
    for copy in copies:
        copy.start()
    total = jnp.zeros((8, channels), jnp.float32)
    squares = jnp.zeros((8, channels), jnp.float32)
    for f in range(frames):
        for r in range(rows):
            copies[f * rows + r].wait()
            value = held[f, r]
            if r == 0:
                edges_ref[0, f, 0] = value
            if r == rows - 1:
                edges_ref[1, f, 0] = value
            wide = value.astype(jnp.float32).reshape(cols // 8, 8, channels)
            total = total + jnp.sum(wide, axis=0)
            squares = squares + jnp.sum(wide * wide, axis=0)
    total = jnp.sum(total, axis=0, keepdims=True)
    squares = jnp.sum(squares, axis=0, keepdims=True)
    for i in range(tiles):
        sums_ref[i : i + 1, :] = total[:, i * LANES : (i + 1) * LANES]
        sums_ref[tiles + i : tiles + i + 1, :] = squares[:, i * LANES : (i + 1) * LANES]


def local_stats(features):
    frames, rows, cols, channels = features.shape
    return pl.pallas_call(
        stats_kernel,
        out_shape=(
            jax.ShapeDtypeStruct((2 * channels // LANES, LANES), jnp.float32),
            jax.ShapeDtypeStruct((2, frames, 1, cols, channels), jnp.bfloat16),
        ),
        in_specs=[pl.BlockSpec(memory_space=pltpu.HBM)],
        scratch_shapes=[
            pltpu.VMEM(features.shape, jnp.bfloat16),
            pltpu.SemaphoreType.DMA((frames * rows,)),
        ],
        cost_estimate=pl.CostEstimate(flops=20_000_000_000, bytes_accessed=features.size * 2, transcendentals=0),
        compiler_params=pltpu.CompilerParams(vmem_limit_bytes=8 * 1024 * 1024),
        name="stats",
    )(features)


def summed_over(value, axis):
    count = lax.axis_size(axis)
    if count & (count - 1):
        return lax.psum(value, axis)
    step = count // 2
    while step:
        value = value + lax.ppermute(value, axis, [(i, i ^ step) for i in range(count)])
        step //= 2
    return value


def moved(value, tm_step, height_step):
    tm, height = lax.axis_size("tm"), lax.axis_size("height")
    pairs = [
        (t * height + h, (t + tm_step) * height + h + height_step)
        for t in range(tm)
        for h in range(height)
        if 0 <= t + tm_step < tm and 0 <= h + height_step < height
    ]
    return lax.ppermute(value, both, pairs)


def coefficients(cells, sums, gain, shift, coef):
    tiles = sums.shape[0] // 2
    per_group = tiles * LANES // GROUPS
    row = lax.broadcasted_iota(jnp.int32, (LANES, LANES), 0) // per_group
    col = lax.broadcasted_iota(jnp.int32, (LANES, LANES), 1) // per_group
    same = jnp.where(row == col, 1.0, 0.0)
    grouped = jnp.dot(
        sums, same, precision=lax.Precision.HIGHEST, preferred_element_type=jnp.float32
    )
    mean = grouped[:tiles] / cells
    var = grouped[tiles:] / cells - mean * mean
    scale = lax.rsqrt(var + epsilon) * gain
    offset = shift - mean * scale
    for i in range(tiles):
        coef[0:1, i * LANES : (i + 1) * LANES] = 0.5 * scale[i : i + 1]
        coef[1:2, i * LANES : (i + 1) * LANES] = 0.5 * offset[i : i + 1]


def activate(raw, act, coef, frames, rows):
    height = lax.axis_index("height")
    top = jnp.where(height == 0, 0.0, 1.0)
    bottom = jnp.where(height == lax.axis_size("height") - 1, 0.0, 1.0)
    half_scale = coef[0:1, :]
    half_offset = coef[1:2, :]
    for f in range(frames):
        for r in range(rows + 2):
            half = raw[f, r].astype(jnp.float32) * half_scale + half_offset
            value = half + half * jnp.tanh(half)
            if r == 0:
                value = value * top
            if r == rows + 1:
                value = value * bottom
            act[f, r] = value.astype(jnp.bfloat16)


def tap_sum(act, weights, slot, first, frames, rows, c):
    cols, channels = act.shape[2:]
    windows = [
        act[first : first + frames, b : b + rows].reshape(frames * rows * cols, channels)
        for b in range(3)
    ]
    return jnp.dot(
        jnp.concatenate(windows, axis=1),
        weights[slot, :, c].reshape(3 * channels, weights.shape[-1]),
        preferred_element_type=jnp.float32,
    )


def own_kernel(
    cells,
    sums_ref,
    gain_ref,
    shift_ref,
    bias_ref,
    own_ref,
    above_ref,
    below_ref,
    kernel_ref,
    out_ref,
    coef,
    raw,
    act,
    acc,
    sem,
):
    frames, rows, cols, _ = own_ref.shape
    cout = out_ref.shape[-1]
    slab = [
        pltpu.make_async_copy(own_ref, raw.at[:, 1 : 1 + rows], sem.at[0]),
        pltpu.make_async_copy(above_ref, raw.at[:, 0:1], sem.at[1]),
        pltpu.make_async_copy(below_ref, raw.at[:, rows + 1 : rows + 2], sem.at[2]),
    ]
    for copy in slab:
        copy.start()
    coefficients(cells, sums_ref[...], gain_ref[...], shift_ref[...], coef)
    for copy in slab:
        copy.wait()
    activate(raw, act, coef, frames, rows)

    for c in range(3):
        newest = tap_sum(act, kernel_ref, 2, 0, frames, rows, c)
        middle = tap_sum(act, kernel_ref, 1, 0, frames - 1, rows, c)
        whole = newest.reshape(frames, rows, cols, cout)
        acc[c, 0] = whole[0]
        acc[c, 1:] = whole[1:] + middle.reshape(frames - 1, rows, cols, cout)
    combine(acc, frames, rows, lambda f, r, value: store(out_ref, f, r, value + bias_ref[...]))


def store(ref, f, r, value):
    ref[f, r] = value.astype(ref.dtype)


def combine(acc, frames, rows, emit):
    cols, cout = acc.shape[3:]
    place = lax.broadcasted_iota(jnp.int32, (cols, cout), 0)
    for f in range(frames):
        for r in range(rows):
            left = jnp.where(place == 0, 0.0, pltpu.roll(acc[0, f, r], 1, 0))
            right = jnp.where(place == cols - 1, 0.0, pltpu.roll(acc[2, f, r], cols - 1, 0))
            emit(f, r, acc[1, f, r] + left + right)


def earlier_kernel(
    coef,
    partial_ref,
    own_ref,
    above_ref,
    below_ref,
    earlier_ref,
    early_above_ref,
    early_below_ref,
    kernel_ref,
    out_ref,
    raw,
    act,
    acc,
    sem,
):
    frames, rows, cols, _ = own_ref.shape
    cout = out_ref.shape[-1]
    tm = lax.axis_index("tm")

    def copies(first):
        out = []
        for i in range(2):
            source = 0 if first else frames - 2 + i
            for j, (ref, start, size) in enumerate(
                (
                    (own_ref if first else earlier_ref, 1, rows),
                    (above_ref if first else early_above_ref, 0, 1),
                    (below_ref if first else early_below_ref, rows + 1, 1),
                )
            ):
                out.append(
                    pltpu.make_async_copy(
                        ref.at[source], raw.at[i, start : start + size], sem.at[3 * i + j]
                    )
                )
        return out

    @pl.when(tm == 0)
    def _():
        for copy in copies(True):
            copy.start()

    @pl.when(tm != 0)
    def _():
        for copy in copies(False):
            copy.start()

    for copy in copies(False):
        copy.wait()
    activate(raw, act, coef, 2, rows)
    for c in range(3):
        oldest = tap_sum(act, kernel_ref, 0, 0, 2, rows, c).reshape(2, rows, cols, cout)
        middle = tap_sum(act, kernel_ref, 1, 1, 1, rows, c).reshape(1, rows, cols, cout)
        acc[c, 0] = oldest[0] + middle[0]
        acc[c, 1] = oldest[1]
    combine(acc, 2, rows, lambda f, r, value: store(out_ref, f, r, value + partial_ref[f, r]))
    for f in range(2, frames):
        for r in range(rows):
            out_ref[f, r] = partial_ref[f, r].astype(jnp.bfloat16)


def on_device(features, gain, shift, kernel, bias):
    frames, rows, cols, channels = features.shape
    cout = kernel.shape[-1]
    tiles = channels // LANES
    cells = lax.axis_size("tm") * lax.axis_size("height") * frames * rows * cols * (channels // GROUPS)
    vmem = pl.BlockSpec(memory_space=pltpu.VMEM)
    anywhere = pl.BlockSpec(memory_space=pl.ANY)
    params = pltpu.CompilerParams(vmem_limit_bytes=32 * 1024 * 1024)
    sums, edges = local_stats(features)
    sums = summed_over(summed_over(sums, "tm"), "height")
    above = moved(edges[1], 0, 1)
    below = moved(edges[0], 0, -1)
    earlier = moved(features, 1, 0)
    early_above = moved(edges[1], 1, 1)
    early_below = moved(edges[0], 1, -1)
    partial, coef = pl.pallas_call(
        functools.partial(own_kernel, float(cells)),
        out_shape=(
            jax.ShapeDtypeStruct((frames, rows, cols, cout), jnp.float32),
            jax.ShapeDtypeStruct((8, channels), jnp.float32),
        ),
        in_specs=[vmem] * 4 + [anywhere] * 3 + [vmem],
        out_specs=(vmem, vmem),
        scratch_shapes=[
            pltpu.VMEM((frames, rows + 2, cols, channels), jnp.bfloat16),
            pltpu.VMEM((frames, rows + 2, cols, channels), jnp.bfloat16),
            pltpu.VMEM((3, frames, rows, cols, cout), jnp.float32),
            pltpu.SemaphoreType.DMA((3,)),
        ],
        compiler_params=params,
        name="own",
    )(
        sums,
        gain.reshape(tiles, LANES),
        shift.reshape(tiles, LANES),
        bias.reshape(1, cout),
        features,
        above,
        below,
        kernel,
    )
    return pl.pallas_call(
        earlier_kernel,
        out_shape=jax.ShapeDtypeStruct((frames, rows, cols, cout), jnp.bfloat16),
        in_specs=[vmem, vmem] + [anywhere] * 6 + [vmem],
        out_specs=vmem,
        scratch_shapes=[
            pltpu.VMEM((2, rows + 2, cols, channels), jnp.bfloat16),
            pltpu.VMEM((2, rows + 2, cols, channels), jnp.bfloat16),
            pltpu.VMEM((3, 2, rows, cols, cout), jnp.float32),
            pltpu.SemaphoreType.DMA((6,)),
        ],
        compiler_params=params,
        name="earlier",
    )(coef, partial, features, above, below, earlier, early_above, early_below, kernel)


def solution(mesh):
    placed = (P(("clips", "tm"), "height", None, None), P(), P(), P(), P())
    tm, height = mesh.shape["tm"], mesh.shape["height"]
    for count in (tm, height):
        step = count // 2
        while step and not count & (count - 1):
            step //= 2
    step = jax.shard_map(
        on_device,
        mesh=mesh,
        in_specs=placed,
        out_specs=P(("clips", "tm"), "height", None, None),
        check_vma=False,
    )
    return step
```

time: 55.2 us -> 43.9 us (0.80)
  waiting for transfers between devices: 9.4 us -> 4.7 us
  local copies, waits for them, and re-layouts: 4.22 us -> 1.17 us
  Pallas kernels: 12.7 us -> 9.7 us
  other arithmetic: 0.7 us -> 0.01 us
    ppermute x5, waiting for transfers between devices: 4.86 us -> 0.38 us  [moved(): return lax.ppermute(value, both, pairs)]
    pallas_call x2 -> x3, Pallas kernels: 12.7 us -> 9.7 us  [the longest x1 4.73 us: on_device(): pl.pallas_call(earlier_kernel, out_shape=jax.ShapeDtypeStruct((frames, ro...]
    unnamed x8 -> x12, local copies, waits for them, and re-layouts: 3.17 us -> 1.14 us
    slice x1 -> x0, local copies, waits for them, and re-layouts: 1.05 us -> none  [on_device(): first_row, last_row = (features[:, :1], features[:, rows - 1:])]
    add x4, other arithmetic: 0.7 us -> 0.01 us  [summed_over(): value + lax.ppermute(value, axis, [(i, i ^ step) for i in range(count)])]
  transfers between devices with their start and end apart: 9 -> 9, of which waited for: 5 -> 4; matrix products, arithmetic and copies ran while one was open for 3% -> 0% of each run, Pallas kernels for 3% -> 11%
where the time goes in v2:
time: 43.9 us; the launch traced here: 43.7 us
  starting transfers between devices  27.9 us (64%)
  Pallas kernels  9.7 us (22%)
  waiting for transfers between devices  4.7 us (11%)
  local copies, waits for them, and re-layouts  1.17 us (3%)
    ppermute x5, starting transfers between devices, moved(): return lax.ppermute(value, both, pairs)  15.9 us
    ppermute x4, starting transfers between devices, summed_over(): lax.ppermute(value, axis, [(i, i ^ step) for i in range(count)])  12 us
    pallas_call x1, Pallas kernels, on_device(): pl.pallas_call(earlier_kernel, out_shape=jax.ShapeDtypeStruct((frames, ro...  4.73 us
    ppermute x4, waiting for transfers between devices, summed_over(): lax.ppermute(value, axis, [(i, i ^ step) for i in range(count)])  4.33 us
    pallas_call x1, Pallas kernels, on_device(): pl.pallas_call(functools.partial(own_kernel, float(cells)), out_shape=(ja...  3.71 us
    pallas_call x1, Pallas kernels, local_stats(): pl.pallas_call(stats_kernel, out_shape=(jax.ShapeDtypeStruct((2 * channel...  1.27 us
    unnamed x12, local copies, waits for them, and re-layouts  1.14 us
  transfers between devices with their start and end apart: 9, of which 4 were waited for; matrix products, arithmetic and copies ran while one was open for 0% of the time, Pallas kernels for 11%

profile of v2, /device:TPU:0, one launch (start us, length us, event | category | flops | bytes accessed | tf_op | source)
XLA Modules:
  0.0 43.7 jit_solution(570935503198278636)
XLA Ops:
  0.0 2.7 %collective-permute-start.6 = (bf16[2,4,96,512]{3,2,1,0:T(8,128)(2,1)}, bf16[2,4,96,512]{3,2,1,0:T(8,128)(2,1)S(1)}, u32[]{:S(2)}, u32[]{:S(2)}) collective-permute-start(bf16[2,4,96,512]{3,2,1,0:T(8,128)(2,1)} %own_ref.3), channel_id=1, source_target_pairs={{0,4},{1,5},{2,6},{3,7},{4,8},{5,9},{6,10},{7,11},{8,12},{9,13},{1... | collective-permute-start | bytes 2359304 | tf_op jit(solution)/shard_map/ppermute | solution.py:85
  2.7 0.0 copy-start.1
  2.7 1.1 %copy-done.1 = bf16[2,4,96,512]{3,2,1,0:T(8,128)(2,1)S(1)} copy-done((bf16[2,4,96,512]{3,2,1,0:T(8,128)(2,1)S(1)}, bf16[2,4,96,512]{3,2,1,0:T(8,128)(2,1)}, u32[]{:S(2)}) %copy-start.1) | copy-done | bytes 786456
  3.9 1.3 %stats.1 = (f32[8,128]{1,0:T(8,128)S(1)}, bf16[2,2,1,96,512]{4,3,2,1,0:T(8,128)(2,1)S(1)}) custom-call(bf16[2,4,96,512]{3,2,1,0:T(8,128)(2,1)S(1)} %copy-done.1), custom_call_target="tpu_custom_call" | custom-call | flops 20000000000 | bytes 786432 | tf_op jit(solution)/shard_map/stats/pallas_call | solution.py:49
  5.1 2.7 %collective-permute-start = (f32[8,128]{1,0:T(8,128)S(1)}, f32[8,128]{1,0:T(8,128)S(1)}, u32[]{:S(2)}, u32[]{:S(2)}) collective-permute-start(f32[8,128]{1,0:T(8,128)S(1)} %get-tuple-element.9), channel_id=1, source_target_pairs={{0,8},{4,12},{8,0},{12,4},{1,9},{5,13},{9,1},{13,5},{2,10},{6,14},... | collective-permute-start | bytes 12296 | tf_op jit(solution)/shard_map/ppermute | solution.py:72
  7.8 1.6 %collective-permute-done = f32[8,128]{1,0:T(8,128)S(1)} collective-permute-done((f32[8,128]{1,0:T(8,128)S(1)}, f32[8,128]{1,0:T(8,128)S(1)}, u32[]{:S(2)}, u32[]{:S(2)}) %collective-permute-start) | collective-permute-done | bytes 4128 | tf_op jit(solution)/shard_map/ppermute | solution.py:72
  9.4 5.2 %collective-permute-start.1 = (f32[8,128]{1,0:T(8,128)S(1)}, f32[8,128]{1,0:T(8,128)S(1)}, u32[]{:S(2)}, u32[]{:S(2)}) collective-permute-start(f32[8,128]{1,0:T(8,128)S(1)} %add.12), channel_id=1, source_target_pairs={{0,4},{4,0},{8,12},{12,8},{1,5},{5,1},{9,13},{13,9},{2,6},{6,2},{1... | collective-permute-start | bytes 12296 | tf_op jit(solution)/shard_map/ppermute | solution.py:72
  14.6 0.8 %collective-permute-done.1 = f32[8,128]{1,0:T(8,128)S(1)} collective-permute-done((f32[8,128]{1,0:T(8,128)S(1)}, f32[8,128]{1,0:T(8,128)S(1)}, u32[]{:S(2)}, u32[]{:S(2)}) %collective-permute-start.1) | collective-permute-done | bytes 4128 | tf_op jit(solution)/shard_map/ppermute | solution.py:72
  15.4 2.6 %collective-permute-start.2 = (f32[8,128]{1,0:T(8,128)S(1)}, f32[8,128]{1,0:T(8,128)S(1)}, u32[]{:S(2)}, u32[]{:S(2)}) collective-permute-start(f32[8,128]{1,0:T(8,128)S(1)} %add.13), channel_id=1, source_target_pairs={{0,2},{1,3},{2,0},{3,1},{4,6},{5,7},{6,4},{7,5},{8,10},{9,11},{10,... | collective-permute-start | bytes 12296 | tf_op jit(solution)/shard_map/ppermute | solution.py:72
  18.0 1.9 %collective-permute-done.2 = f32[8,128]{1,0:T(8,128)S(1)} collective-permute-done((f32[8,128]{1,0:T(8,128)S(1)}, f32[8,128]{1,0:T(8,128)S(1)}, u32[]{:S(2)}, u32[]{:S(2)}) %collective-permute-start.2) | collective-permute-done | bytes 4128 | tf_op jit(solution)/shard_map/ppermute | solution.py:72
  19.9 1.6 %collective-permute-start.3 = (f32[8,128]{1,0:T(8,128)S(1)}, f32[8,128]{1,0:T(8,128)S(1)}, u32[]{:S(2)}, u32[]{:S(2)}) collective-permute-start(f32[8,128]{1,0:T(8,128)S(1)} %add.14), channel_id=1, source_target_pairs={{0,1},{1,0},{2,3},{3,2},{4,5},{5,4},{6,7},{7,6},{8,9},{9,8},{10,11... | collective-permute-start | bytes 12296 | tf_op jit(solution)/shard_map/ppermute | solution.py:72
  21.5 1.3 %collective-permute-start.5 = (bf16[2,1,96,512]{3,2,1,0:T(8,128)(2,1)S(1)}, bf16[2,1,96,512]{3,2,1,0:T(8,128)(2,1)S(1)}, u32[]{:S(2)}, u32[]{:S(2)}) collective-permute-start(bf16[2,1,96,512]{3,2,1,0:T(8,128)(2,1)S(1)} %get-tuple-element.13), channel_id=1, source_target_pairs={{1,0},{2,1},{3,2},{5,4},{6,5},{7,6},{9,8},{10,9},{11,10},{13,12},{... | collective-permute-start | bytes 589832 | tf_op jit(solution)/shard_map/ppermute | solution.py:85
  22.8 4.6 %collective-permute-start.4 = (bf16[2,1,96,512]{3,2,1,0:T(8,128)(2,1)S(1)}, bf16[2,1,96,512]{3,2,1,0:T(8,128)(2,1)S(1)}, u32[]{:S(2)}, u32[]{:S(2)}) collective-permute-start(bf16[2,1,96,512]{3,2,1,0:T(8,128)(2,1)S(1)} %get-tuple-element.14), channel_id=1, source_target_pairs={{0,1},{1,2},{2,3},{4,5},{5,6},{6,7},{8,9},{9,10},{10,11},{12,13},{... | collective-permute-start | bytes 589832 | tf_op jit(solution)/shard_map/ppermute | solution.py:85
  27.4 0.7 %collective-permute-start.8 = (bf16[2,1,96,512]{3,2,1,0:T(8,128)(2,1)S(1)}, bf16[2,1,96,512]{3,2,1,0:T(8,128)(2,1)S(1)}, u32[]{:S(2)}, u32[]{:S(2)}) collective-permute-start(bf16[2,1,96,512]{3,2,1,0:T(8,128)(2,1)S(1)} %get-tuple-element.13), channel_id=1, source_target_pairs={{1,4},{2,5},{3,6},{5,8},{6,9},{7,10},{9,12},{10,13},{11,14},{17,20... | collective-permute-start | bytes 589832 | tf_op jit(solution)/shard_map/ppermute | solution.py:85
  28.0 0.0 collective-permute-done.3
  28.1 6.7 %collective-permute-start.7 = (bf16[2,1,96,512]{3,2,1,0:T(8,128)(2,1)S(1)}, bf16[2,1,96,512]{3,2,1,0:T(8,128)(2,1)S(1)}, u32[]{:S(2)}, u32[]{:S(2)}) collective-permute-start(bf16[2,1,96,512]{3,2,1,0:T(8,128)(2,1)S(1)} %get-tuple-element.14), channel_id=1, source_target_pairs={{0,5},{1,6},{2,7},{4,9},{5,10},{6,11},{8,13},{9,14},{10,15},{16,21... | collective-permute-start | bytes 589832 | tf_op jit(solution)/shard_map/ppermute | solution.py:85
  34.8 0.0 collective-permute-done.5.below_ref
  34.8 0.0 collective-permute-done.4.above_ref
  34.8 0.0 copy-done
  34.9 3.7 %own.1 = (f32[2,4,96,256]{3,2,1,0:T(8,128)S(1)}, f32[8,512]{1,0:T(8,128)S(1)}) custom-call(f32[8,128]{1,0:T(8,128)S(1)} %add.15.sums_ref, f32[4,128]{1,0:T(4,128)S(1)} %bitcast.9, f32[4,128]{1,0:T(4,128)S(1)} %bitcast.10, f32[1,256]{1,0:T(1,128)S(1)} %bitcast.11, bf16[2,4,96,512]{3,2,1,0:T(8,128)(2,1)S(1)} %copy-done.2, ...), custom_call_target="tpu_custom_call" | custom-call | tf_op jit(solution)/shard_map/own/pallas_call | solution.py:267
  38.6 0.0 collective-permute-done.8.early_below_ref
  38.6 0.4 collective-permute-done.7.early_above_ref
  38.9 0.0 collective-permute-done.6.earlier_ref
  39.0 4.7 %earlier.1 = bf16[2,4,96,256]{3,2,1,0:T(8,128)(2,1)} custom-call(f32[8,512]{1,0:T(8,128)S(1)} %get-tuple-element.11.coef, f32[2,4,96,256]{3,2,1,0:T(8,128)S(1)} %get-tuple-element.12.partial_ref, bf16[2,4,96,512]{3,2,1,0:T(8,128)(2,1)S(1)} %copy-done.2, bf16[2,1,96,512]{3,2,1,0:T(8,128)(2,1)S(1)} %collective-permute-done.4.above_ref, ...), custom_call_target="tpu_custom_call" | custom-call | tf_op jit(solution)/shard_map/earlier/pallas_call | solution.py:293
  (14 shorter events, 0.1 us)
Async XLA Ops:
  0.0 34.8 %copy-start = (bf16[3,3,3,512,256]{4,3,2,1,0:T(8,128)(2,1)S(1)}, bf16[3,3,3,512,256]{4,3,2,1,0:T(8,128)(2,1)}, u32[]{:S(2)}) copy-start(bf16[3,3,3,512,256]{4,3,2,1,0:T(8,128)(2,1)} %kernel_ref.3) | copy-start | bytes 21233668
  0.0 38.9 %collective-permute-start.6 = (bf16[2,4,96,512]{3,2,1,0:T(8,128)(2,1)}, bf16[2,4,96,512]{3,2,1,0:T(8,128)(2,1)S(1)}, u32[]{:S(2)}, u32[]{:S(2)}) collective-permute-start(bf16[2,4,96,512]{3,2,1,0:T(8,128)(2,1)} %own_ref.3), channel_id=1, source_target_pairs={{0,4},{1,5},{2,6},{3,7},{4,8},{5,9},{6,10},{7,11},{8,12},{9,13},{1... | collective-permute-start | bytes 2359304 | tf_op jit(solution)/shard_map/ppermute | solution.py:85
  2.7 1.1 %copy-start.1 = (bf16[2,4,96,512]{3,2,1,0:T(8,128)(2,1)S(1)}, bf16[2,4,96,512]{3,2,1,0:T(8,128)(2,1)}, u32[]{:S(2)}) copy-start(bf16[2,4,96,512]{3,2,1,0:T(8,128)(2,1)} %own_ref.3) | copy-start | bytes 2359300
  3.8 31.0 %copy-start.2 = (bf16[2,4,96,512]{3,2,1,0:T(8,128)(2,1)S(1)}, bf16[2,4,96,512]{3,2,1,0:T(8,128)(2,1)}, u32[]{:S(2)}) copy-start(bf16[2,4,96,512]{3,2,1,0:T(8,128)(2,1)} %own_ref.3) | copy-start | bytes 2359300
  3.8 31.0 %copy-start.3 = (f32[512]{0:T(512)S(1)}, f32[512]{0:T(512)}, u32[]{:S(2)}) copy-start(f32[512]{0:T(512)} %param.6) | copy-start | bytes 6148
  3.8 31.0 %copy-start.4 = (f32[512]{0:T(512)S(1)}, f32[512]{0:T(512)}, u32[]{:S(2)}) copy-start(f32[512]{0:T(512)} %param.7) | copy-start | bytes 6148
  3.8 31.0 %copy-start.5 = (f32[256]{0:T(256)S(1)}, f32[256]{0:T(256)}, u32[]{:S(2)}) copy-start(f32[256]{0:T(256)} %param.9) | copy-start | bytes 3076
  5.1 4.3 %collective-permute-start = (f32[8,128]{1,0:T(8,128)S(1)}, f32[8,128]{1,0:T(8,128)S(1)}, u32[]{:S(2)}, u32[]{:S(2)}) collective-permute-start(f32[8,128]{1,0:T(8,128)S(1)} %get-tuple-element.9), channel_id=1, source_target_pairs={{0,8},{4,12},{8,0},{12,4},{1,9},{5,13},{9,1},{13,5},{2,10},{6,14},... | collective-permute-start | bytes 12296 | tf_op jit(solution)/shard_map/ppermute | solution.py:72
  9.4 6.0 %collective-permute-start.1 = (f32[8,128]{1,0:T(8,128)S(1)}, f32[8,128]{1,0:T(8,128)S(1)}, u32[]{:S(2)}, u32[]{:S(2)}) collective-permute-start(f32[8,128]{1,0:T(8,128)S(1)} %add.12), channel_id=1, source_target_pairs={{0,4},{4,0},{8,12},{12,8},{1,5},{5,1},{9,13},{13,9},{2,6},{6,2},{1... | collective-permute-start | bytes 12296 | tf_op jit(solution)/shard_map/ppermute | solution.py:72
  15.4 4.5 %collective-permute-start.2 = (f32[8,128]{1,0:T(8,128)S(1)}, f32[8,128]{1,0:T(8,128)S(1)}, u32[]{:S(2)}, u32[]{:S(2)}) collective-permute-start(f32[8,128]{1,0:T(8,128)S(1)} %add.13), channel_id=1, source_target_pairs={{0,2},{1,3},{2,0},{3,1},{4,6},{5,7},{6,4},{7,5},{8,10},{9,11},{10,... | collective-permute-start | bytes 12296 | tf_op jit(solution)/shard_map/ppermute | solution.py:72
  19.9 8.2 %collective-permute-start.3 = (f32[8,128]{1,0:T(8,128)S(1)}, f32[8,128]{1,0:T(8,128)S(1)}, u32[]{:S(2)}, u32[]{:S(2)}) collective-permute-start(f32[8,128]{1,0:T(8,128)S(1)} %add.14), channel_id=1, source_target_pairs={{0,1},{1,0},{2,3},{3,2},{4,5},{5,4},{6,7},{7,6},{8,9},{9,8},{10,11... | collective-permute-start | bytes 12296 | tf_op jit(solution)/shard_map/ppermute | solution.py:72
  21.5 13.3 %collective-permute-start.5 = (bf16[2,1,96,512]{3,2,1,0:T(8,128)(2,1)S(1)}, bf16[2,1,96,512]{3,2,1,0:T(8,128)(2,1)S(1)}, u32[]{:S(2)}, u32[]{:S(2)}) collective-permute-start(bf16[2,1,96,512]{3,2,1,0:T(8,128)(2,1)S(1)} %get-tuple-element.13), channel_id=1, source_target_pairs={{1,0},{2,1},{3,2},{5,4},{6,5},{7,6},{9,8},{10,9},{11,10},{13,12},{... | collective-permute-start | bytes 589832 | tf_op jit(solution)/shard_map/ppermute | solution.py:85
  22.8 12.0 %collective-permute-start.4 = (bf16[2,1,96,512]{3,2,1,0:T(8,128)(2,1)S(1)}, bf16[2,1,96,512]{3,2,1,0:T(8,128)(2,1)S(1)}, u32[]{:S(2)}, u32[]{:S(2)}) collective-permute-start(bf16[2,1,96,512]{3,2,1,0:T(8,128)(2,1)S(1)} %get-tuple-element.14), channel_id=1, source_target_pairs={{0,1},{1,2},{2,3},{4,5},{5,6},{6,7},{8,9},{9,10},{10,11},{12,13},{... | collective-permute-start | bytes 589832 | tf_op jit(solution)/shard_map/ppermute | solution.py:85
  27.4 11.2 %collective-permute-start.8 = (bf16[2,1,96,512]{3,2,1,0:T(8,128)(2,1)S(1)}, bf16[2,1,96,512]{3,2,1,0:T(8,128)(2,1)S(1)}, u32[]{:S(2)}, u32[]{:S(2)}) collective-permute-start(bf16[2,1,96,512]{3,2,1,0:T(8,128)(2,1)S(1)} %get-tuple-element.13), channel_id=1, source_target_pairs={{1,4},{2,5},{3,6},{5,8},{6,9},{7,10},{9,12},{10,13},{11,14},{17,20... | collective-permute-start | bytes 589832 | tf_op jit(solution)/shard_map/ppermute | solution.py:85
  28.1 10.9 %collective-permute-start.7 = (bf16[2,1,96,512]{3,2,1,0:T(8,128)(2,1)S(1)}, bf16[2,1,96,512]{3,2,1,0:T(8,128)(2,1)S(1)}, u32[]{:S(2)}, u32[]{:S(2)}) collective-permute-start(bf16[2,1,96,512]{3,2,1,0:T(8,128)(2,1)S(1)} %get-tuple-element.14), channel_id=1, source_target_pairs={{0,5},{1,6},{2,7},{4,9},{5,10},{6,11},{8,13},{9,14},{10,15},{16,21... | collective-permute-start | bytes 589832 | tf_op jit(solution)/shard_map/ppermute | solution.py:85

commit v3 on v2

--- a/solution.py
+++ b/solution.py
@@ -11,10 +11,9 @@
 GROUPS = 32
 LANES = 128
 epsilon = 1e-06
-both = ("tm", "height")
-
-
-def stats_kernel(x_ref, sums_ref, edges_ref, held, sem):
+
+
+def stats_kernel(x_ref, sums_ref, edge_a_ref, edge_b_ref, held, sem):
     frames, rows, cols, channels = x_ref.shape
     tiles = channels // LANES
     copies = [
@@ -29,14 +28,13 @@
     for f in range(frames):
         for r in range(rows):
             copies[f * rows + r].wait()
-            value = held[f, r]
-            if r == 0:
-                edges_ref[0, f, 0] = value
-            if r == rows - 1:
-                edges_ref[1, f, 0] = value
-            wide = value.astype(jnp.float32).reshape(cols // 8, 8, channels)
+            wide = held[f, r].astype(jnp.float32).reshape(cols // 8, 8, channels)
             total = total + jnp.sum(wide, axis=0)
             squares = squares + jnp.sum(wide * wide, axis=0)
+    odd = lax.axis_index("height") % 2
+    for f in range(frames):
+        edge_a_ref[f] = held[f, (rows - 1) * (1 - odd)]
+        edge_b_ref[f] = held[f, (rows - 1) * odd]
     total = jnp.sum(total, axis=0, keepdims=True)
     squares = jnp.sum(squares, axis=0, keepdims=True)
     for i in range(tiles):
@@ -50,7 +48,8 @@
         stats_kernel,
         out_shape=(
             jax.ShapeDtypeStruct((2 * channels // LANES, LANES), jnp.float32),
-            jax.ShapeDtypeStruct((2, frames, 1, cols, channels), jnp.bfloat16),
+            jax.ShapeDtypeStruct((frames, cols, channels), jnp.bfloat16),
+            jax.ShapeDtypeStruct((frames, cols, channels), jnp.bfloat16),
         ),
         in_specs=[pl.BlockSpec(memory_space=pltpu.HBM)],
         scratch_shapes=[
@@ -60,7 +59,7 @@
         cost_estimate=pl.CostEstimate(flops=20_000_000_000, bytes_accessed=features.size * 2, transcendentals=0),
         compiler_params=pltpu.CompilerParams(vmem_limit_bytes=8 * 1024 * 1024),
         name="stats",
-    )(features)
+    )(pltpu.with_memory_space_constraint(features, pltpu.HBM))
 
 
 def summed_over(value, axis):
@@ -74,15 +73,18 @@
     return value
 
 
-def moved(value, tm_step, height_step):
-    tm, height = lax.axis_size("tm"), lax.axis_size("height")
-    pairs = [
-        (t * height + h, (t + tm_step) * height + h + height_step)
-        for t in range(tm)
-        for h in range(height)
-        if 0 <= t + tm_step < tm and 0 <= h + height_step < height
-    ]
-    return lax.ppermute(value, both, pairs)
+def shifted(value):
+    return lax.ppermute(value, "tm", [(i, i + 1) for i in range(lax.axis_size("tm") - 1)])
+
+
+def swapped(value, start):
+    pairs = [(i, i + 1) for i in range(start, lax.axis_size("height") - 1, 2)]
+    return lax.ppermute(value, "height", pairs + [(j, i) for i, j in pairs])
+
+
+def edge_slots(rows):
+    odd = lax.axis_index("height") % 2
+    return (rows + 1) * (1 - odd), (rows + 1) * odd
 
 
 def coefficients(cells, sums, gain, shift, coef):
@@ -140,8 +142,8 @@
     shift_ref,
     bias_ref,
     own_ref,
-    above_ref,
-    below_ref,
+    edge_a_ref,
+    edge_b_ref,
     kernel_ref,
     out_ref,
     coef,
@@ -152,10 +154,11 @@
 ):
     frames, rows, cols, _ = own_ref.shape
     cout = out_ref.shape[-1]
+    slot_a, slot_b = edge_slots(rows)
     slab = [
         pltpu.make_async_copy(own_ref, raw.at[:, 1 : 1 + rows], sem.at[0]),
-        pltpu.make_async_copy(above_ref, raw.at[:, 0:1], sem.at[1]),
-        pltpu.make_async_copy(below_ref, raw.at[:, rows + 1 : rows + 2], sem.at[2]),
+        pltpu.make_async_copy(edge_a_ref, raw.at[:, slot_a], sem.at[1]),
+        pltpu.make_async_copy(edge_b_ref, raw.at[:, slot_b], sem.at[2]),
     ]
     for copy in slab:
         copy.start()
@@ -191,11 +194,10 @@
     coef,
     partial_ref,
     own_ref,
-    above_ref,
-    below_ref,
+    edge_a_ref,
+    edge_b_ref,
     earlier_ref,
-    early_above_ref,
-    early_below_ref,
+    corners_ref,
     kernel_ref,
     out_ref,
     raw,
@@ -207,22 +209,19 @@
     cout = out_ref.shape[-1]
     tm = lax.axis_index("tm")
 
+    slot_a, slot_b = edge_slots(rows)
+
     def copies(first):
         out = []
         for i in range(2):
-            source = 0 if first else frames - 2 + i
-            for j, (ref, start, size) in enumerate(
-                (
-                    (own_ref if first else earlier_ref, 1, rows),
-                    (above_ref if first else early_above_ref, 0, 1),
-                    (below_ref if first else early_below_ref, rows + 1, 1),
-                )
-            ):
-                out.append(
-                    pltpu.make_async_copy(
-                        ref.at[source], raw.at[i, start : start + size], sem.at[3 * i + j]
-                    )
-                )
+            sources = (
+                (own_ref.at[0], edge_a_ref.at[0], edge_b_ref.at[0])
+                if first
+                else (earlier_ref.at[i], corners_ref.at[i], corners_ref.at[2 + i])
+            )
+            targets = raw.at[i, 1 : 1 + rows], raw.at[i, slot_a], raw.at[i, slot_b]
+            for j in range(3):
+                out.append(pltpu.make_async_copy(sources[j], targets[j], sem.at[3 * i + j]))
         return out
 
     @pl.when(tm == 0)
@@ -257,13 +256,12 @@
     vmem = pl.BlockSpec(memory_space=pltpu.VMEM)
     anywhere = pl.BlockSpec(memory_space=pl.ANY)
     params = pltpu.CompilerParams(vmem_limit_bytes=32 * 1024 * 1024)
-    sums, edges = local_stats(features)
+    sums, edge_a, edge_b = local_stats(features)
     sums = summed_over(summed_over(sums, "tm"), "height")
-    above = moved(edges[1], 0, 1)
-    below = moved(edges[0], 0, -1)
-    earlier = moved(features, 1, 0)
-    early_above = moved(edges[1], 1, 1)
-    early_below = moved(edges[0], 1, -1)
+    edge_a = swapped(edge_a, 0)
+    edge_b = swapped(edge_b, 1)
+    earlier = shifted(features[frames - 2 :])
+    corners = shifted(jnp.concatenate([edge_a[frames - 2 :], edge_b[frames - 2 :]]))
     partial, coef = pl.pallas_call(
         functools.partial(own_kernel, float(cells)),
         out_shape=(
@@ -286,14 +284,14 @@
         shift.reshape(tiles, LANES),
         bias.reshape(1, cout),
         features,
-        above,
-        below,
+        edge_a,
+        edge_b,
         kernel,
     )
     return pl.pallas_call(
         earlier_kernel,
         out_shape=jax.ShapeDtypeStruct((frames, rows, cols, cout), jnp.bfloat16),
-        in_specs=[vmem, vmem] + [anywhere] * 6 + [vmem],
+        in_specs=[vmem, vmem] + [anywhere] * 5 + [vmem],
         out_specs=vmem,
         scratch_shapes=[
             pltpu.VMEM((2, rows + 2, cols, channels), jnp.bfloat16),
@@ -303,7 +301,7 @@
         ],
         compiler_params=params,
         name="earlier",
-    )(coef, partial, features, above, below, earlier, early_above, early_below, kernel)
+    )(coef, partial, features, edge_a, edge_b, earlier, corners, kernel)
 
 
 def solution(mesh):

time: 43.9 us -> 40.7 us (0.927)
  the two profiles are of different devices: /device:TPU:0 before, /device:TPU:4 now
where the time goes in v3:
time: 40.7 us; the launch traced here: 40 us
  starting transfers between devices  18.8 us (46%)
  waiting for transfers between devices  11.2 us (28%)
  Pallas kernels  9.79 us (24%)
    ppermute x4, starting transfers between devices, summed_over(): lax.ppermute(value, axis, [(i, i ^ step) for i in range(count)])  12.2 us
    ppermute x4, waiting for transfers between devices, summed_over(): lax.ppermute(value, axis, [(i, i ^ step) for i in range(count)])  6.88 us
    pallas_call x1, Pallas kernels, on_device(): pl.pallas_call(earlier_kernel, out_shape=jax.ShapeDtypeStruct((frames, ro...  4.75 us
    ppermute x2, waiting for transfers between devices, swapped(): return lax.ppermute(value, 'height', pairs + [(j, i) for i, j in pairs])  4.33 us
    ppermute x2, starting transfers between devices, shifted(): lax.ppermute(value, 'tm', [(i, i + 1) for i in range(lax.axis_size('tm')...  4.24 us
    pallas_call x1, Pallas kernels, on_device(): pl.pallas_call(functools.partial(own_kernel, float(cells)), out_shape=(ja...  3.72 us
    ppermute x2, starting transfers between devices, swapped(): return lax.ppermute(value, 'height', pairs + [(j, i) for i, j in pairs])  2.3 us
    pallas_call x1, Pallas kernels, local_stats(): pl.pallas_call(stats_kernel, out_shape=(jax.ShapeDtypeStruct((2 * channel...  1.32 us
  transfers between devices with their start and end apart: 8, of which 5 were waited for; matrix products, arithmetic and copies ran while one was open for 0% of the time, Pallas kernels for 13%

profile of v3, /device:TPU:4, one launch (start us, length us, event | category | flops | bytes accessed | tf_op | source)
XLA Modules:
  0.0 40.0 jit_solution(4629516970546746160)
XLA Ops:
  0.0 0.0 copy-start.3
  0.0 0.0 copy-start.2
  0.0 2.3 %collective-permute-start.6 = (bf16[2,4,96,512]{3,2,1,0:T(8,128)(2,1)}, bf16[2,4,96,512]{3,2,1,0:T(8,128)(2,1)S(1)}, u32[]{:S(2)}, u32[]{:S(2)}) collective-permute-start(bf16[2,4,96,512]{3,2,1,0:T(8,128)(2,1)} %own_ref.3), channel_id=1, source_target_pairs={{0,4},{4,8},{8,12},{1,5},{5,9},{9,13},{2,6},{6,10},{10,14},{3,7},{... | collective-permute-start | bytes 2359304 | tf_op jit(solution)/shard_map/ppermute | solution.py:77
  2.4 1.3 %stats.1 = (f32[8,128]{1,0:T(8,128)S(1)}, bf16[2,96,512]{2,1,0:T(8,128)(2,1)S(1)}, bf16[2,96,512]{2,1,0:T(8,128)(2,1)S(1)}) custom-call(bf16[2,4,96,512]{3,2,1,0:T(8,128)(2,1)} %own_ref.3), custom_call_target="tpu_custom_call" | custom-call | flops 20000000000 | bytes 786432 | tf_op jit(solution)/shard_map/stats/pallas_call | solution.py:47
  3.7 1.6 %collective-permute-start.4 = (bf16[2,96,512]{2,1,0:T(8,128)(2,1)S(1)}, bf16[2,96,512]{2,1,0:T(8,128)(2,1)S(1)}, u32[]{:S(2)}, u32[]{:S(2)}) collective-permute-start(bf16[2,96,512]{2,1,0:T(8,128)(2,1)S(1)} %get-tuple-element.11), channel_id=1, source_target_pairs={{0,1},{2,3},{1,0},{3,2},{4,5},{6,7},{5,4},{7,6},{8,9},{10,11},{9,8... | collective-permute-start | bytes 589832 | tf_op jit(solution)/shard_map/ppermute | solution.py:82
  5.3 0.7 %collective-permute-start.5 = (bf16[2,96,512]{2,1,0:T(8,128)(2,1)S(1)}, bf16[2,96,512]{2,1,0:T(8,128)(2,1)S(1)}, u32[]{:S(2)}, u32[]{:S(2)}) collective-permute-start(bf16[2,96,512]{2,1,0:T(8,128)(2,1)S(1)} %get-tuple-element.12), channel_id=1, source_target_pairs={{1,2},{2,1},{5,6},{6,5},{9,10},{10,9},{13,14},{14,13},{17,18},{18,... | collective-permute-start | bytes 589832 | tf_op jit(solution)/shard_map/ppermute | solution.py:82
  6.0 4.3 %collective-permute-done.4.edge_a_ref = bf16[2,96,512]{2,1,0:T(8,128)(2,1)S(1)} collective-permute-done((bf16[2,96,512]{2,1,0:T(8,128)(2,1)S(1)}, bf16[2,96,512]{2,1,0:T(8,128)(2,1)S(1)}, u32[]{:S(2)}, u32[]{:S(2)}) %collective-permute-start.4) | collective-permute-done | bytes 196640 | tf_op jit(solution)/shard_map/ppermute | solution.py:82
  10.3 0.0 collective-permute-done.5.edge_b_ref
  10.4 1.9 %collective-permute-start.7 = (bf16[4,96,512]{2,1,0:T(8,128)(2,1)S(1)}, bf16[4,96,512]{2,1,0:T(8,128)(2,1)S(1)}, u32[]{:S(2)}, u32[]{:S(2)}) collective-permute-start(bf16[4,96,512]{2,1,0:T(8,128)(2,1)S(1)} %pad_maximum_fusion), channel_id=1, source_target_pairs={{0,4},{4,8},{8,12},{1,5},{5,9},{9,13},{2,6},{6,10},{10,14},{3,7},{... | collective-permute-start | bytes 1179656 | tf_op jit(solution)/shard_map/ppermute | solution.py:77
  12.3 1.1 %collective-permute-start = (f32[8,128]{1,0:T(8,128)S(1)}, f32[8,128]{1,0:T(8,128)S(1)}, u32[]{:S(2)}, u32[]{:S(2)}) collective-permute-start(f32[8,128]{1,0:T(8,128)S(1)} %get-tuple-element.10), channel_id=1, source_target_pairs={{0,8},{4,12},{8,0},{12,4},{1,9},{5,13},{9,1},{13,5},{2,10},{6,14},... | collective-permute-start | bytes 12296 | tf_op jit(solution)/shard_map/ppermute | solution.py:71
  13.4 2.6 %collective-permute-done = f32[8,128]{1,0:T(8,128)S(1)} collective-permute-done((f32[8,128]{1,0:T(8,128)S(1)}, f32[8,128]{1,0:T(8,128)S(1)}, u32[]{:S(2)}, u32[]{:S(2)}) %collective-permute-start) | collective-permute-done | bytes 4128 | tf_op jit(solution)/shard_map/ppermute | solution.py:71
  16.0 3.6 %collective-permute-start.1 = (f32[8,128]{1,0:T(8,128)S(1)}, f32[8,128]{1,0:T(8,128)S(1)}, u32[]{:S(2)}, u32[]{:S(2)}) collective-permute-start(f32[8,128]{1,0:T(8,128)S(1)} %add.12), channel_id=1, source_target_pairs={{0,4},{4,0},{8,12},{12,8},{1,5},{5,1},{9,13},{13,9},{2,6},{6,2},{1... | collective-permute-start | bytes 12296 | tf_op jit(solution)/shard_map/ppermute | solution.py:71
  19.6 0.8 %collective-permute-done.1 = f32[8,128]{1,0:T(8,128)S(1)} collective-permute-done((f32[8,128]{1,0:T(8,128)S(1)}, f32[8,128]{1,0:T(8,128)S(1)}, u32[]{:S(2)}, u32[]{:S(2)}) %collective-permute-start.1) | collective-permute-done | bytes 4128 | tf_op jit(solution)/shard_map/ppermute | solution.py:71
  20.5 5.8 %collective-permute-start.2 = (f32[8,128]{1,0:T(8,128)S(1)}, f32[8,128]{1,0:T(8,128)S(1)}, u32[]{:S(2)}, u32[]{:S(2)}) collective-permute-start(f32[8,128]{1,0:T(8,128)S(1)} %add.13), channel_id=1, source_target_pairs={{0,2},{1,3},{2,0},{3,1},{4,6},{5,7},{6,4},{7,5},{8,10},{9,11},{10,... | collective-permute-start | bytes 12296 | tf_op jit(solution)/shard_map/ppermute | solution.py:71
  26.2 1.6 %collective-permute-done.2 = f32[8,128]{1,0:T(8,128)S(1)} collective-permute-done((f32[8,128]{1,0:T(8,128)S(1)}, f32[8,128]{1,0:T(8,128)S(1)}, u32[]{:S(2)}, u32[]{:S(2)}) %collective-permute-start.2) | collective-permute-done | bytes 4128 | tf_op jit(solution)/shard_map/ppermute | solution.py:71
  27.8 1.8 %collective-permute-start.3 = (f32[8,128]{1,0:T(8,128)S(1)}, f32[8,128]{1,0:T(8,128)S(1)}, u32[]{:S(2)}, u32[]{:S(2)}) collective-permute-start(f32[8,128]{1,0:T(8,128)S(1)} %add.14), channel_id=1, source_target_pairs={{0,1},{1,0},{2,3},{3,2},{4,5},{5,4},{6,7},{7,6},{8,9},{9,8},{10,11... | collective-permute-start | bytes 12296 | tf_op jit(solution)/shard_map/ppermute | solution.py:71
  29.6 1.9 %collective-permute-done.3 = f32[8,128]{1,0:T(8,128)S(1)} collective-permute-done((f32[8,128]{1,0:T(8,128)S(1)}, f32[8,128]{1,0:T(8,128)S(1)}, u32[]{:S(2)}, u32[]{:S(2)}) %collective-permute-start.3) | collective-permute-done | bytes 4128 | tf_op jit(solution)/shard_map/ppermute | solution.py:71
  31.4 0.0 copy-done.1
  31.4 0.0 copy-done
  31.4 0.0 copy-done.4
  31.5 3.7 %own.1 = (f32[2,4,96,256]{3,2,1,0:T(8,128)S(1)}, f32[8,512]{1,0:T(8,128)S(1)}) custom-call(f32[8,128]{1,0:T(8,128)S(1)} %add.15.sums_ref, f32[4,128]{1,0:T(4,128)S(1)} %bitcast.3, f32[4,128]{1,0:T(4,128)S(1)} %bitcast.4, f32[1,256]{1,0:T(1,128)S(1)} %bitcast.5, bf16[2,4,96,512]{3,2,1,0:T(8,128)(2,1)S(1)} %copy-done.1, ...), custom_call_target="tpu_custom_call" | custom-call | tf_op jit(solution)/shard_map/own/pallas_call | solution.py:265
  35.2 0.0 collective-permute-done.7.corners_ref
  35.2 0.0 collective-permute-done.6.earlier_ref
  35.2 4.7 %earlier.1 = bf16[2,4,96,256]{3,2,1,0:T(8,128)(2,1)} custom-call(f32[8,512]{1,0:T(8,128)S(1)} %get-tuple-element.13.coef, f32[2,4,96,256]{3,2,1,0:T(8,128)S(1)} %get-tuple-element.14.partial_ref, bf16[2,4,96,512]{3,2,1,0:T(8,128)(2,1)S(1)} %copy-done.1, bf16[2,96,512]{2,1,0:T(8,128)(2,1)S(1)} %collective-permute-done.4.edge_a_ref, ...), custom_call_target="tpu_custom_call" | custom-call | tf_op jit(solution)/shard_map/earlier/pallas_call | solution.py:291
  (10 shorter events, 0.1 us)
Async XLA Ops:
  0.0 31.4 %copy-start.1 = (bf16[2,4,96,512]{3,2,1,0:T(8,128)(2,1)S(1)}, bf16[2,4,96,512]{3,2,1,0:T(8,128)(2,1)}, u32[]{:S(2)}) copy-start(bf16[2,4,96,512]{3,2,1,0:T(8,128)(2,1)} %own_ref.3) | copy-start | bytes 2359300
  0.0 31.4 %copy-start = (bf16[3,3,3,512,256]{4,3,2,1,0:T(8,128)(2,1)S(1)}, bf16[3,3,3,512,256]{4,3,2,1,0:T(8,128)(2,1)}, u32[]{:S(2)}) copy-start(bf16[3,3,3,512,256]{4,3,2,1,0:T(8,128)(2,1)} %kernel_ref.3) | copy-start | bytes 21233668
  0.0 31.4 %copy-start.4 = (f32[256]{0:T(256)S(1)}, f32[256]{0:T(256)}, u32[]{:S(2)}) copy-start(f32[256]{0:T(256)} %param.9) | copy-start | bytes 3076
  0.0 31.4 %copy-start.3 = (f32[512]{0:T(512)S(1)}, f32[512]{0:T(512)}, u32[]{:S(2)}) copy-start(f32[512]{0:T(512)} %param.7) | copy-start | bytes 6148
  0.0 31.4 %copy-start.2 = (f32[512]{0:T(512)S(1)}, f32[512]{0:T(512)}, u32[]{:S(2)}) copy-start(f32[512]{0:T(512)} %param.6) | copy-start | bytes 6148
  0.0 35.2 %collective-permute-start.6 = (bf16[2,4,96,512]{3,2,1,0:T(8,128)(2,1)}, bf16[2,4,96,512]{3,2,1,0:T(8,128)(2,1)S(1)}, u32[]{:S(2)}, u32[]{:S(2)}) collective-permute-start(bf16[2,4,96,512]{3,2,1,0:T(8,128)(2,1)} %own_ref.3), channel_id=1, source_target_pairs={{0,4},{4,8},{8,12},{1,5},{5,9},{9,13},{2,6},{6,10},{10,14},{3,7},{... | collective-permute-start | bytes 2359304 | tf_op jit(solution)/shard_map/ppermute | solution.py:77
  3.7 6.6 %collective-permute-start.4 = (bf16[2,96,512]{2,1,0:T(8,128)(2,1)S(1)}, bf16[2,96,512]{2,1,0:T(8,128)(2,1)S(1)}, u32[]{:S(2)}, u32[]{:S(2)}) collective-permute-start(bf16[2,96,512]{2,1,0:T(8,128)(2,1)S(1)} %get-tuple-element.11), channel_id=1, source_target_pairs={{0,1},{2,3},{1,0},{3,2},{4,5},{6,7},{5,4},{7,6},{8,9},{10,11},{9,8... | collective-permute-start | bytes 589832 | tf_op jit(solution)/shard_map/ppermute | solution.py:82
  5.3 5.0 %collective-permute-start.5 = (bf16[2,96,512]{2,1,0:T(8,128)(2,1)S(1)}, bf16[2,96,512]{2,1,0:T(8,128)(2,1)S(1)}, u32[]{:S(2)}, u32[]{:S(2)}) collective-permute-start(bf16[2,96,512]{2,1,0:T(8,128)(2,1)S(1)} %get-tuple-element.12), channel_id=1, source_target_pairs={{1,2},{2,1},{5,6},{6,5},{9,10},{10,9},{13,14},{14,13},{17,18},{18,... | collective-permute-start | bytes 589832 | tf_op jit(solution)/shard_map/ppermute | solution.py:82
  10.4 24.8 %collective-permute-start.7 = (bf16[4,96,512]{2,1,0:T(8,128)(2,1)S(1)}, bf16[4,96,512]{2,1,0:T(8,128)(2,1)S(1)}, u32[]{:S(2)}, u32[]{:S(2)}) collective-permute-start(bf16[4,96,512]{2,1,0:T(8,128)(2,1)S(1)} %pad_maximum_fusion), channel_id=1, source_target_pairs={{0,4},{4,8},{8,12},{1,5},{5,9},{9,13},{2,6},{6,10},{10,14},{3,7},{... | collective-permute-start | bytes 1179656 | tf_op jit(solution)/shard_map/ppermute | solution.py:77
  12.3 3.7 %collective-permute-start = (f32[8,128]{1,0:T(8,128)S(1)}, f32[8,128]{1,0:T(8,128)S(1)}, u32[]{:S(2)}, u32[]{:S(2)}) collective-permute-start(f32[8,128]{1,0:T(8,128)S(1)} %get-tuple-element.10), channel_id=1, source_target_pairs={{0,8},{4,12},{8,0},{12,4},{1,9},{5,13},{9,1},{13,5},{2,10},{6,14},... | collective-permute-start | bytes 12296 | tf_op jit(solution)/shard_map/ppermute | solution.py:71
  16.0 4.4 %collective-permute-start.1 = (f32[8,128]{1,0:T(8,128)S(1)}, f32[8,128]{1,0:T(8,128)S(1)}, u32[]{:S(2)}, u32[]{:S(2)}) collective-permute-start(f32[8,128]{1,0:T(8,128)S(1)} %add.12), channel_id=1, source_target_pairs={{0,4},{4,0},{8,12},{12,8},{1,5},{5,1},{9,13},{13,9},{2,6},{6,2},{1... | collective-permute-start | bytes 12296 | tf_op jit(solution)/shard_map/ppermute | solution.py:71
  20.5 7.3 %collective-permute-start.2 = (f32[8,128]{1,0:T(8,128)S(1)}, f32[8,128]{1,0:T(8,128)S(1)}, u32[]{:S(2)}, u32[]{:S(2)}) collective-permute-start(f32[8,128]{1,0:T(8,128)S(1)} %add.13), channel_id=1, source_target_pairs={{0,2},{1,3},{2,0},{3,1},{4,6},{5,7},{6,4},{7,5},{8,10},{9,11},{10,... | collective-permute-start | bytes 12296 | tf_op jit(solution)/shard_map/ppermute | solution.py:71
  27.8 3.6 %collective-permute-start.3 = (f32[8,128]{1,0:T(8,128)S(1)}, f32[8,128]{1,0:T(8,128)S(1)}, u32[]{:S(2)}, u32[]{:S(2)}) collective-permute-start(f32[8,128]{1,0:T(8,128)S(1)} %add.14), channel_id=1, source_target_pairs={{0,1},{1,0},{2,3},{3,2},{4,5},{5,4},{6,7},{7,6},{8,9},{9,8},{10,11... | collective-permute-start | bytes 12296 | tf_op jit(solution)/shard_map/ppermute | solution.py:71

commit v4 on v3

v4 whole, which is shorter than its diff:
```python
import functools

import jax
import jax.numpy as jnp
from jax import lax
from jax.experimental import pallas as pl
from jax.experimental.pallas import tpu as pltpu
from jax.sharding import PartitionSpec as P


GROUPS = 32
LANES = 128
epsilon = 1e-06


def stats_kernel(x_ref, sums_ref, edge_a_ref, edge_b_ref, held, sem):
    frames, rows, cols, channels = x_ref.shape
    tiles = channels // LANES
    copies = [
        pltpu.make_async_copy(x_ref.at[f, r], held.at[f, r], sem.at[f * rows + r])
        for f in range(frames)
        for r in range(rows)
    ]
    for copy in copies:
        copy.start()
    total = jnp.zeros((8, channels), jnp.float32)
    squares = jnp.zeros((8, channels), jnp.float32)
    for f in range(frames):
        for r in range(rows):
            copies[f * rows + r].wait()
            wide = held[f, r].astype(jnp.float32).reshape(cols // 8, 8, channels)
            total = total + jnp.sum(wide, axis=0)
            squares = squares + jnp.sum(wide * wide, axis=0)
    odd = lax.axis_index("height") % 2
    for f in range(frames):
        edge_a_ref[f] = held[f, (rows - 1) * (1 - odd)]
        edge_b_ref[f] = held[f, (rows - 1) * odd]
    total = jnp.sum(total, axis=0, keepdims=True)
    squares = jnp.sum(squares, axis=0, keepdims=True)
    for i in range(tiles):
        sums_ref[i : i + 1, :] = total[:, i * LANES : (i + 1) * LANES]
        sums_ref[tiles + i : tiles + i + 1, :] = squares[:, i * LANES : (i + 1) * LANES]


def local_stats(features):
    frames, rows, cols, channels = features.shape
    return pl.pallas_call(
        stats_kernel,
        out_shape=(
            jax.ShapeDtypeStruct((2 * channels // LANES, LANES), jnp.float32),
            jax.ShapeDtypeStruct((frames, cols, channels), jnp.bfloat16),
            jax.ShapeDtypeStruct((frames, cols, channels), jnp.bfloat16),
        ),
        in_specs=[pl.BlockSpec(memory_space=pltpu.HBM)],
        scratch_shapes=[
            pltpu.VMEM(features.shape, jnp.bfloat16),
            pltpu.SemaphoreType.DMA((frames * rows,)),
        ],
        cost_estimate=pl.CostEstimate(flops=20_000_000_000, bytes_accessed=features.size * 2, transcendentals=0),
        compiler_params=pltpu.CompilerParams(vmem_limit_bytes=8 * 1024 * 1024),
        name="stats",
    )(pltpu.with_memory_space_constraint(features, pltpu.HBM))


def summed_over(value, axis):
    count = lax.axis_size(axis)
    if count & (count - 1):
        return lax.psum(value, axis)
    step = count // 2
    while step:
        value = value + lax.ppermute(value, axis, [(i, i ^ step) for i in range(count)])
        step //= 2
    return value


def shifted(value):
    return lax.ppermute(value, "tm", [(i, i + 1) for i in range(lax.axis_size("tm") - 1)])


def swapped(value, start):
    pairs = [(i, i + 1) for i in range(start, lax.axis_size("height") - 1, 2)]
    return lax.ppermute(value, "height", pairs + [(j, i) for i, j in pairs])


def coefficients(cells, sums, gain, shift, coef):
    tiles = sums.shape[0] // 2
    per_group = tiles * LANES // GROUPS
    row = lax.broadcasted_iota(jnp.int32, (LANES, LANES), 0) // per_group
    col = lax.broadcasted_iota(jnp.int32, (LANES, LANES), 1) // per_group
    same = jnp.where(row == col, 1.0, 0.0)
    grouped = jnp.dot(
        sums, same, precision=lax.Precision.HIGHEST, preferred_element_type=jnp.float32
    )
    mean = grouped[:tiles] / cells
    var = grouped[tiles:] / cells - mean * mean
    scale = lax.rsqrt(var + epsilon) * gain
    offset = shift - mean * scale
    for i in range(tiles):
        coef[0:1, i * LANES : (i + 1) * LANES] = 0.5 * scale[i : i + 1]
        coef[1:2, i * LANES : (i + 1) * LANES] = 0.5 * offset[i : i + 1]


def activate(source, act, coef, edge, rows):
    half_scale = coef[0:1, :]
    half_offset = coef[1:2, :]
    for r in range(rows + 2):
        half = source(r).astype(jnp.float32) * half_scale + half_offset
        value = half + half * jnp.tanh(half)
        if r == 0:
            value = value * edge[0]
        if r == rows + 1:
            value = value * edge[1]
        act[r] = value.astype(jnp.bfloat16)


def edge_masks():
    height = lax.axis_index("height")
    return (
        jnp.where(height == 0, 0.0, 1.0),
        jnp.where(height == lax.axis_size("height") - 1, 0.0, 1.0),
    )


def tap_sum(slabs, kernel_ref, first, rows, emit):
    cols, channels = slabs[0].shape[1:]
    cout = kernel_ref.shape[-1]
    taps = slice(first, first + len(slabs))

    def product(c):
        windows = [
            slab[b : b + rows].reshape(rows * cols, channels) for slab in slabs for b in range(3)
        ]
        return jnp.dot(
            jnp.concatenate(windows, axis=1),
            kernel_ref[taps, :, c].reshape(len(slabs) * 3 * channels, cout),
            preferred_element_type=jnp.float32,
        ).reshape(rows, cols, cout)

    left, right, middle = product(0), product(2), product(1)
    place = lax.broadcasted_iota(jnp.int32, (cols, cout), 0)
    for r in range(rows):
        from_left = jnp.where(place == 0, 0.0, pltpu.roll(left[r], 1, 0))
        from_right = jnp.where(place == cols - 1, 0.0, pltpu.roll(right[r], cols - 1, 0))
        emit(r, middle[r] + from_left + from_right)


def own_kernel(
    cells,
    sums_ref,
    gain_ref,
    shift_ref,
    bias_ref,
    own_ref,
    edge_a_ref,
    edge_b_ref,
    kernel_ref,
    out_ref,
    coef,
    *acts,
):
    frames, rows = own_ref.shape[:2]
    odd = lax.axis_index("height") % 2 == 1
    edge = edge_masks()
    coefficients(cells, sums_ref[...], gain_ref[...], shift_ref[...], coef)

    def source(f):
        def row(r):
            if r == 0:
                return jnp.where(odd, edge_a_ref[f], edge_b_ref[f])
            if r == rows + 1:
                return jnp.where(odd, edge_b_ref[f], edge_a_ref[f])
            return own_ref[f, r - 1]

        return row

    for f in range(frames):
        activate(source(f), acts[f], coef, edge, rows)

        def emit(r, value, f=f):
            out_ref[f, r] = value + bias_ref[...]

        tap_sum(acts[max(0, f - 2) : f + 1], kernel_ref, max(0, 2 - f), rows, emit)


def earlier_kernel(
    coef,
    partial_ref,
    own_ref,
    edge_a_ref,
    edge_b_ref,
    earlier_ref,
    corners_ref,
    kernel_ref,
    out_ref,
    old_act,
    new_act,
    staged,
    sem,
):
    frames, rows = own_ref.shape[:2]
    odd = lax.axis_index("height") % 2 == 1
    start = lax.axis_index("tm") == 0
    edge = edge_masks()

    def source(i):
        def row(r):
            if 0 < r <= rows:
                return jnp.where(start, own_ref[0, r - 1], earlier_ref[i, r - 1])
            a = jnp.where(start, edge_a_ref[0], corners_ref[i])
            b = jnp.where(start, edge_b_ref[0], corners_ref[2 + i])
            return jnp.where(odd, a, b) if r == 0 else jnp.where(odd, b, a)

        return row

    copies = []

    def finish(f, slabs, first):
        if slabs:

            def emit(r, value):
                staged[f, r] = (value + partial_ref[f, r]).astype(jnp.bfloat16)

            tap_sum(slabs, kernel_ref, first, rows, emit)
        else:
            for r in range(rows):
                staged[f, r] = partial_ref[f, r].astype(jnp.bfloat16)
        copy = pltpu.make_async_copy(staged.at[f], out_ref.at[f], sem.at[f])
        copy.start()
        copies.append(copy)

    for f in range(2, frames):
        finish(f, (), 0)
    activate(source(1), new_act, coef, edge, rows)
    finish(1, (new_act,), 0)
    activate(source(0), old_act, coef, edge, rows)
    finish(0, (old_act, new_act), 0)
    for copy in copies:
        copy.wait()


def on_device(features, gain, shift, kernel, bias):
    frames, rows, cols, channels = features.shape
    cout = kernel.shape[-1]
    tiles = channels // LANES
    cells = lax.axis_size("tm") * lax.axis_size("height") * frames * rows * cols * (channels // GROUPS)
    vmem = pl.BlockSpec(memory_space=pltpu.VMEM)
    params = pltpu.CompilerParams(vmem_limit_bytes=32 * 1024 * 1024)
    sums, edge_a, edge_b = local_stats(features)
    sums = summed_over(summed_over(sums, "tm"), "height")
    edge_a = swapped(edge_a, 0)
    edge_b = swapped(edge_b, 1)
    earlier = shifted(features[frames - 2 :])
    corners = shifted(jnp.concatenate([edge_a[frames - 2 :], edge_b[frames - 2 :]]))
    partial, coef = pl.pallas_call(
        functools.partial(own_kernel, float(cells)),
        out_shape=(
            jax.ShapeDtypeStruct((frames, rows, cols, cout), jnp.float32),
            jax.ShapeDtypeStruct((8, channels), jnp.float32),
        ),
        in_specs=[vmem] * 8,
        out_specs=(vmem, vmem),
        scratch_shapes=[pltpu.VMEM((rows + 2, cols, channels), jnp.bfloat16)] * frames,
        compiler_params=params,
        name="own",
    )(
        sums,
        gain.reshape(tiles, LANES),
        shift.reshape(tiles, LANES),
        bias.reshape(1, cout),
        features,
        edge_a,
        edge_b,
        kernel,
    )
    return pl.pallas_call(
        earlier_kernel,
        out_shape=jax.ShapeDtypeStruct((frames, rows, cols, cout), jnp.bfloat16),
        in_specs=[vmem] * 8,
        out_specs=pl.BlockSpec(memory_space=pltpu.HBM),
        scratch_shapes=[
            pltpu.VMEM((rows + 2, cols, channels), jnp.bfloat16),
            pltpu.VMEM((rows + 2, cols, channels), jnp.bfloat16),
            pltpu.VMEM((frames, rows, cols, cout), jnp.bfloat16),
            pltpu.SemaphoreType.DMA((frames,)),
        ],
        compiler_params=params,
        name="earlier",
    )(coef, partial, features, edge_a, edge_b, earlier, corners, kernel)


def solution(mesh):
    placed = (P(("clips", "tm"), "height", None, None), P(), P(), P(), P())
    tm, height = mesh.shape["tm"], mesh.shape["height"]
    for count in (tm, height):
        step = count // 2
        while step and not count & (count - 1):
            step //= 2
    step = jax.shard_map(
        on_device,
        mesh=mesh,
        in_specs=placed,
        out_specs=P(("clips", "tm"), "height", None, None),
        check_vma=False,
    )
    return step
```

time: 40.7 us -> 39.1 us (0.961)
  Pallas kernels: 9.79 us -> 8.23 us
    pallas_call x1, Pallas kernels: 4.75 us -> 3.69 us  [on_device(): pl.pallas_call(earlier_kernel, out_shape=jax.ShapeDtypeStruct((frames, ro...]
    pallas_call x1, Pallas kernels: 3.72 us -> 3.22 us  [on_device(): pl.pallas_call(functools.partial(own_kernel, float(cells)), out_shape=(ja...]
  transfers between devices with their start and end apart: 8 -> 8, of which waited for: 5 -> 5; matrix products, arithmetic and copies ran while one was open for 0% -> 0% of each run, Pallas kernels for 13% -> 12%
where the time goes in v4:
time: 39.1 us; the launch traced here: 38.4 us
  starting transfers between devices  18.8 us (48%)
  waiting for transfers between devices  11.2 us (29%)
  Pallas kernels  8.23 us (21%)
    ppermute x4, starting transfers between devices, summed_over(): lax.ppermute(value, axis, [(i, i ^ step) for i in range(count)])  12.2 us
    ppermute x4, waiting for transfers between devices, summed_over(): lax.ppermute(value, axis, [(i, i ^ step) for i in range(count)])  6.88 us
    ppermute x2, waiting for transfers between devices, swapped(): return lax.ppermute(value, 'height', pairs + [(j, i) for i, j in pairs])  4.33 us
    ppermute x2, starting transfers between devices, shifted(): lax.ppermute(value, 'tm', [(i, i + 1) for i in range(lax.axis_size('tm')...  4.24 us
    pallas_call x1, Pallas kernels, on_device(): pl.pallas_call(earlier_kernel, out_shape=jax.ShapeDtypeStruct((frames, ro...  3.69 us
    pallas_call x1, Pallas kernels, on_device(): pl.pallas_call(functools.partial(own_kernel, float(cells)), out_shape=(ja...  3.22 us
    ppermute x2, starting transfers between devices, swapped(): return lax.ppermute(value, 'height', pairs + [(j, i) for i, j in pairs])  2.3 us
    pallas_call x1, Pallas kernels, local_stats(): pl.pallas_call(stats_kernel, out_shape=(jax.ShapeDtypeStruct((2 * channel...  1.32 us
  transfers between devices with their start and end apart: 8, of which 5 were waited for; matrix products, arithmetic and copies ran while one was open for 0% of the time, Pallas kernels for 12%

profile of v4, /device:TPU:4, one launch (start us, length us, event | category | flops | bytes accessed | tf_op | source)
XLA Modules:
  0.0 38.4 jit_solution(7807348830424548474)
XLA Ops:
  0.0 0.0 copy-start.3
  0.0 0.0 copy-start.2
  0.0 2.3 %collective-permute-start.6 = (bf16[2,4,96,512]{3,2,1,0:T(8,128)(2,1)}, bf16[2,4,96,512]{3,2,1,0:T(8,128)(2,1)S(1)}, u32[]{:S(2)}, u32[]{:S(2)}) collective-permute-start(bf16[2,4,96,512]{3,2,1,0:T(8,128)(2,1)} %own_ref.3), channel_id=1, source_target_pairs={{0,4},{4,8},{8,12},{1,5},{5,9},{9,13},{2,6},{6,10},{10,14},{3,7},{... | collective-permute-start | bytes 2359304 | tf_op jit(solution)/shard_map/ppermute | solution.py:77
  2.4 1.3 %stats.1 = (f32[8,128]{1,0:T(8,128)S(1)}, bf16[2,96,512]{2,1,0:T(8,128)(2,1)S(1)}, bf16[2,96,512]{2,1,0:T(8,128)(2,1)S(1)}) custom-call(bf16[2,4,96,512]{3,2,1,0:T(8,128)(2,1)} %own_ref.3), custom_call_target="tpu_custom_call" | custom-call | flops 20000000000 | bytes 786432 | tf_op jit(solution)/shard_map/stats/pallas_call | solution.py:47
  3.7 1.6 %collective-permute-start.4 = (bf16[2,96,512]{2,1,0:T(8,128)(2,1)S(1)}, bf16[2,96,512]{2,1,0:T(8,128)(2,1)S(1)}, u32[]{:S(2)}, u32[]{:S(2)}) collective-permute-start(bf16[2,96,512]{2,1,0:T(8,128)(2,1)S(1)} %get-tuple-element.11), channel_id=1, source_target_pairs={{0,1},{2,3},{1,0},{3,2},{4,5},{6,7},{5,4},{7,6},{8,9},{10,11},{9,8... | collective-permute-start | bytes 589832 | tf_op jit(solution)/shard_map/ppermute | solution.py:82
  5.3 0.7 %collective-permute-start.5 = (bf16[2,96,512]{2,1,0:T(8,128)(2,1)S(1)}, bf16[2,96,512]{2,1,0:T(8,128)(2,1)S(1)}, u32[]{:S(2)}, u32[]{:S(2)}) collective-permute-start(bf16[2,96,512]{2,1,0:T(8,128)(2,1)S(1)} %get-tuple-element.12), channel_id=1, source_target_pairs={{1,2},{2,1},{5,6},{6,5},{9,10},{10,9},{13,14},{14,13},{17,18},{18,... | collective-permute-start | bytes 589832 | tf_op jit(solution)/shard_map/ppermute | solution.py:82
  6.0 4.3 %collective-permute-done.4.edge_a_ref = bf16[2,96,512]{2,1,0:T(8,128)(2,1)S(1)} collective-permute-done((bf16[2,96,512]{2,1,0:T(8,128)(2,1)S(1)}, bf16[2,96,512]{2,1,0:T(8,128)(2,1)S(1)}, u32[]{:S(2)}, u32[]{:S(2)}) %collective-permute-start.4) | collective-permute-done | bytes 196640 | tf_op jit(solution)/shard_map/ppermute | solution.py:82
  10.3 0.0 collective-permute-done.5.edge_b_ref
  10.4 1.9 %collective-permute-start.7 = (bf16[4,96,512]{2,1,0:T(8,128)(2,1)S(1)}, bf16[4,96,512]{2,1,0:T(8,128)(2,1)S(1)}, u32[]{:S(2)}, u32[]{:S(2)}) collective-permute-start(bf16[4,96,512]{2,1,0:T(8,128)(2,1)S(1)} %pad_maximum_fusion), channel_id=1, source_target_pairs={{0,4},{4,8},{8,12},{1,5},{5,9},{9,13},{2,6},{6,10},{10,14},{3,7},{... | collective-permute-start | bytes 1179656 | tf_op jit(solution)/shard_map/ppermute | solution.py:77
  12.3 1.1 %collective-permute-start = (f32[8,128]{1,0:T(8,128)S(1)}, f32[8,128]{1,0:T(8,128)S(1)}, u32[]{:S(2)}, u32[]{:S(2)}) collective-permute-start(f32[8,128]{1,0:T(8,128)S(1)} %get-tuple-element.10), channel_id=1, source_target_pairs={{0,8},{4,12},{8,0},{12,4},{1,9},{5,13},{9,1},{13,5},{2,10},{6,14},... | collective-permute-start | bytes 12296 | tf_op jit(solution)/shard_map/ppermute | solution.py:71
  13.4 2.6 %collective-permute-done = f32[8,128]{1,0:T(8,128)S(1)} collective-permute-done((f32[8,128]{1,0:T(8,128)S(1)}, f32[8,128]{1,0:T(8,128)S(1)}, u32[]{:S(2)}, u32[]{:S(2)}) %collective-permute-start) | collective-permute-done | bytes 4128 | tf_op jit(solution)/shard_map/ppermute | solution.py:71
  16.0 3.6 %collective-permute-start.1 = (f32[8,128]{1,0:T(8,128)S(1)}, f32[8,128]{1,0:T(8,128)S(1)}, u32[]{:S(2)}, u32[]{:S(2)}) collective-permute-start(f32[8,128]{1,0:T(8,128)S(1)} %add.12), channel_id=1, source_target_pairs={{0,4},{4,0},{8,12},{12,8},{1,5},{5,1},{9,13},{13,9},{2,6},{6,2},{1... | collective-permute-start | bytes 12296 | tf_op jit(solution)/shard_map/ppermute | solution.py:71
  19.6 0.8 %collective-permute-done.1 = f32[8,128]{1,0:T(8,128)S(1)} collective-permute-done((f32[8,128]{1,0:T(8,128)S(1)}, f32[8,128]{1,0:T(8,128)S(1)}, u32[]{:S(2)}, u32[]{:S(2)}) %collective-permute-start.1) | collective-permute-done | bytes 4128 | tf_op jit(solution)/shard_map/ppermute | solution.py:71
  20.5 5.8 %collective-permute-start.2 = (f32[8,128]{1,0:T(8,128)S(1)}, f32[8,128]{1,0:T(8,128)S(1)}, u32[]{:S(2)}, u32[]{:S(2)}) collective-permute-start(f32[8,128]{1,0:T(8,128)S(1)} %add.13), channel_id=1, source_target_pairs={{0,2},{1,3},{2,0},{3,1},{4,6},{5,7},{6,4},{7,5},{8,10},{9,11},{10,... | collective-permute-start | bytes 12296 | tf_op jit(solution)/shard_map/ppermute | solution.py:71
  26.2 1.6 %collective-permute-done.2 = f32[8,128]{1,0:T(8,128)S(1)} collective-permute-done((f32[8,128]{1,0:T(8,128)S(1)}, f32[8,128]{1,0:T(8,128)S(1)}, u32[]{:S(2)}, u32[]{:S(2)}) %collective-permute-start.2) | collective-permute-done | bytes 4128 | tf_op jit(solution)/shard_map/ppermute | solution.py:71
  27.8 1.8 %collective-permute-start.3 = (f32[8,128]{1,0:T(8,128)S(1)}, f32[8,128]{1,0:T(8,128)S(1)}, u32[]{:S(2)}, u32[]{:S(2)}) collective-permute-start(f32[8,128]{1,0:T(8,128)S(1)} %add.14), channel_id=1, source_target_pairs={{0,1},{1,0},{2,3},{3,2},{4,5},{5,4},{6,7},{7,6},{8,9},{9,8},{10,11... | collective-permute-start | bytes 12296 | tf_op jit(solution)/shard_map/ppermute | solution.py:71
  29.6 1.9 %collective-permute-done.3 = f32[8,128]{1,0:T(8,128)S(1)} collective-permute-done((f32[8,128]{1,0:T(8,128)S(1)}, f32[8,128]{1,0:T(8,128)S(1)}, u32[]{:S(2)}, u32[]{:S(2)}) %collective-permute-start.3) | collective-permute-done | bytes 4128 | tf_op jit(solution)/shard_map/ppermute | solution.py:71
  31.4 0.0 copy-done.1
  31.4 0.0 copy-done
  31.4 0.0 copy-done.4
  31.5 3.2 %own.1 = (f32[2,4,96,256]{3,2,1,0:T(8,128)S(1)}, f32[8,512]{1,0:T(8,128)S(1)}) custom-call(f32[8,128]{1,0:T(8,128)S(1)} %add.15.sums_ref, f32[4,128]{1,0:T(4,128)S(1)} %bitcast.3, f32[4,128]{1,0:T(4,128)S(1)} %bitcast.4, f32[1,256]{1,0:T(1,128)S(1)} %bitcast.5, bf16[2,4,96,512]{3,2,1,0:T(8,128)(2,1)S(1)} %copy-done.1, ...), custom_call_target="tpu_custom_call" | custom-call | tf_op jit(solution)/shard_map/own/pallas_call | solution.py:254
  34.7 0.0 collective-permute-done.7.corners_ref
  34.7 0.0 collective-permute-done.6.earlier_ref
  34.7 3.7 %earlier.1 = bf16[2,4,96,256]{3,2,1,0:T(8,128)(2,1)} custom-call(f32[8,512]{1,0:T(8,128)S(1)} %get-tuple-element.13.coef, f32[2,4,96,256]{3,2,1,0:T(8,128)S(1)} %get-tuple-element.14.partial_ref, bf16[2,4,96,512]{3,2,1,0:T(8,128)(2,1)S(1)} %copy-done.1, bf16[2,96,512]{2,1,0:T(8,128)(2,1)S(1)} %collective-permute-done.4.edge_a_ref, ...), custom_call_target="tpu_custom_call" | custom-call | tf_op jit(solution)/shard_map/earlier/pallas_call | solution.py:275
  (10 shorter events, 0.1 us)
Async XLA Ops:
  0.0 31.4 %copy-start.1 = (bf16[2,4,96,512]{3,2,1,0:T(8,128)(2,1)S(1)}, bf16[2,4,96,512]{3,2,1,0:T(8,128)(2,1)}, u32[]{:S(2)}) copy-start(bf16[2,4,96,512]{3,2,1,0:T(8,128)(2,1)} %own_ref.3) | copy-start | bytes 2359300
  0.0 31.4 %copy-start = (bf16[3,3,3,512,256]{4,3,2,1,0:T(8,128)(2,1)S(1)}, bf16[3,3,3,512,256]{4,3,2,1,0:T(8,128)(2,1)}, u32[]{:S(2)}) copy-start(bf16[3,3,3,512,256]{4,3,2,1,0:T(8,128)(2,1)} %kernel_ref.3) | copy-start | bytes 21233668
  0.0 31.4 %copy-start.4 = (f32[256]{0:T(256)S(1)}, f32[256]{0:T(256)}, u32[]{:S(2)}) copy-start(f32[256]{0:T(256)} %param.9) | copy-start | bytes 3076
  0.0 31.4 %copy-start.3 = (f32[512]{0:T(512)S(1)}, f32[512]{0:T(512)}, u32[]{:S(2)}) copy-start(f32[512]{0:T(512)} %param.7) | copy-start | bytes 6148
  0.0 31.4 %copy-start.2 = (f32[512]{0:T(512)S(1)}, f32[512]{0:T(512)}, u32[]{:S(2)}) copy-start(f32[512]{0:T(512)} %param.6) | copy-start | bytes 6148
  0.0 34.7 %collective-permute-start.6 = (bf16[2,4,96,512]{3,2,1,0:T(8,128)(2,1)}, bf16[2,4,96,512]{3,2,1,0:T(8,128)(2,1)S(1)}, u32[]{:S(2)}, u32[]{:S(2)}) collective-permute-start(bf16[2,4,96,512]{3,2,1,0:T(8,128)(2,1)} %own_ref.3), channel_id=1, source_target_pairs={{0,4},{4,8},{8,12},{1,5},{5,9},{9,13},{2,6},{6,10},{10,14},{3,7},{... | collective-permute-start | bytes 2359304 | tf_op jit(solution)/shard_map/ppermute | solution.py:77
  3.7 6.6 %collective-permute-start.4 = (bf16[2,96,512]{2,1,0:T(8,128)(2,1)S(1)}, bf16[2,96,512]{2,1,0:T(8,128)(2,1)S(1)}, u32[]{:S(2)}, u32[]{:S(2)}) collective-permute-start(bf16[2,96,512]{2,1,0:T(8,128)(2,1)S(1)} %get-tuple-element.11), channel_id=1, source_target_pairs={{0,1},{2,3},{1,0},{3,2},{4,5},{6,7},{5,4},{7,6},{8,9},{10,11},{9,8... | collective-permute-start | bytes 589832 | tf_op jit(solution)/shard_map/ppermute | solution.py:82
  5.3 5.0 %collective-permute-start.5 = (bf16[2,96,512]{2,1,0:T(8,128)(2,1)S(1)}, bf16[2,96,512]{2,1,0:T(8,128)(2,1)S(1)}, u32[]{:S(2)}, u32[]{:S(2)}) collective-permute-start(bf16[2,96,512]{2,1,0:T(8,128)(2,1)S(1)} %get-tuple-element.12), channel_id=1, source_target_pairs={{1,2},{2,1},{5,6},{6,5},{9,10},{10,9},{13,14},{14,13},{17,18},{18,... | collective-permute-start | bytes 589832 | tf_op jit(solution)/shard_map/ppermute | solution.py:82
  10.4 24.3 %collective-permute-start.7 = (bf16[4,96,512]{2,1,0:T(8,128)(2,1)S(1)}, bf16[4,96,512]{2,1,0:T(8,128)(2,1)S(1)}, u32[]{:S(2)}, u32[]{:S(2)}) collective-permute-start(bf16[4,96,512]{2,1,0:T(8,128)(2,1)S(1)} %pad_maximum_fusion), channel_id=1, source_target_pairs={{0,4},{4,8},{8,12},{1,5},{5,9},{9,13},{2,6},{6,10},{10,14},{3,7},{... | collective-permute-start | bytes 1179656 | tf_op jit(solution)/shard_map/ppermute | solution.py:77
  12.3 3.7 %collective-permute-start = (f32[8,128]{1,0:T(8,128)S(1)}, f32[8,128]{1,0:T(8,128)S(1)}, u32[]{:S(2)}, u32[]{:S(2)}) collective-permute-start(f32[8,128]{1,0:T(8,128)S(1)} %get-tuple-element.10), channel_id=1, source_target_pairs={{0,8},{4,12},{8,0},{12,4},{1,9},{5,13},{9,1},{13,5},{2,10},{6,14},... | collective-permute-start | bytes 12296 | tf_op jit(solution)/shard_map/ppermute | solution.py:71
  16.0 4.4 %collective-permute-start.1 = (f32[8,128]{1,0:T(8,128)S(1)}, f32[8,128]{1,0:T(8,128)S(1)}, u32[]{:S(2)}, u32[]{:S(2)}) collective-permute-start(f32[8,128]{1,0:T(8,128)S(1)} %add.12), channel_id=1, source_target_pairs={{0,4},{4,0},{8,12},{12,8},{1,5},{5,1},{9,13},{13,9},{2,6},{6,2},{1... | collective-permute-start | bytes 12296 | tf_op jit(solution)/shard_map/ppermute | solution.py:71
  20.5 7.3 %collective-permute-start.2 = (f32[8,128]{1,0:T(8,128)S(1)}, f32[8,128]{1,0:T(8,128)S(1)}, u32[]{:S(2)}, u32[]{:S(2)}) collective-permute-start(f32[8,128]{1,0:T(8,128)S(1)} %add.13), channel_id=1, source_target_pairs={{0,2},{1,3},{2,0},{3,1},{4,6},{5,7},{6,4},{7,5},{8,10},{9,11},{10,... | collective-permute-start | bytes 12296 | tf_op jit(solution)/shard_map/ppermute | solution.py:71
  27.8 3.6 %collective-permute-start.3 = (f32[8,128]{1,0:T(8,128)S(1)}, f32[8,128]{1,0:T(8,128)S(1)}, u32[]{:S(2)}, u32[]{:S(2)}) collective-permute-start(f32[8,128]{1,0:T(8,128)S(1)} %add.14), channel_id=1, source_target_pairs={{0,1},{1,0},{2,3},{3,2},{4,5},{5,4},{6,7},{7,6},{8,9},{9,8},{10,11... | collective-permute-start | bytes 12296 | tf_op jit(solution)/shard_map/ppermute | solution.py:71

commit v5 on v4

--- a/solution.py
+++ b/solution.py
@@ -62,14 +62,17 @@
     )(pltpu.with_memory_space_constraint(features, pltpu.HBM))
 
 
+def round_steps(count):
+    steps = [1 << i for i in range(count.bit_length() - 1)]
+    return steps
+
+
 def summed_over(value, axis):
     count = lax.axis_size(axis)
     if count & (count - 1):
         return lax.psum(value, axis)
-    step = count // 2
-    while step:
+    for step in round_steps(count):
         value = value + lax.ppermute(value, axis, [(i, i ^ step) for i in range(count)])
-        step //= 2
     return value
 
 
@@ -290,16 +293,10 @@
 
 def solution(mesh):
     placed = (P(("clips", "tm"), "height", None, None), P(), P(), P(), P())
-    tm, height = mesh.shape["tm"], mesh.shape["height"]
-    for count in (tm, height):
-        step = count // 2
-        while step and not count & (count - 1):
-            step //= 2
-    step = jax.shard_map(
+    return jax.shard_map(
         on_device,
         mesh=mesh,
         in_specs=placed,
         out_specs=P(("clips", "tm"), "height", None, None),
         check_vma=False,
     )
-    return step

time: 39.1 us -> 38.1 us (0.974)
  the two profiles are of different devices: /device:TPU:4 before, /device:TPU:0 now
where the time goes in v5:
time: 38.1 us; the launch traced here: 37.9 us
  starting transfers between devices  18.2 us (48%)
  waiting for transfers between devices  11.3 us (30%)
  Pallas kernels  8.23 us (22%)
    ppermute x4, starting transfers between devices, summed_over(): lax.ppermute(value, axis, [(i, i ^ step) for i in range(count)])  9.34 us
    ppermute x4, waiting for transfers between devices, summed_over(): lax.ppermute(value, axis, [(i, i ^ step) for i in range(count)])  7.26 us
    ppermute x2, starting transfers between devices, shifted(): lax.ppermute(value, 'tm', [(i, i + 1) for i in range(lax.axis_size('tm')...  5.64 us
    ppermute x2, waiting for transfers between devices, swapped(): return lax.ppermute(value, 'height', pairs + [(j, i) for i, j in pairs])  4.06 us
    pallas_call x1, Pallas kernels, on_device(): pl.pallas_call(earlier_kernel, out_shape=jax.ShapeDtypeStruct((frames, ro...  3.69 us
    pallas_call x1, Pallas kernels, on_device(): pl.pallas_call(functools.partial(own_kernel, float(cells)), out_shape=(ja...  3.22 us
    ppermute x2, starting transfers between devices, swapped(): return lax.ppermute(value, 'height', pairs + [(j, i) for i, j in pairs])  3.19 us
    pallas_call x1, Pallas kernels, local_stats(): pl.pallas_call(stats_kernel, out_shape=(jax.ShapeDtypeStruct((2 * channel...  1.32 us
  transfers between devices with their start and end apart: 8, of which 5 were waited for; matrix products, arithmetic and copies ran while one was open for 0% of the time, Pallas kernels for 12%

profile of v5, /device:TPU:0, one launch (start us, length us, event | category | flops | bytes accessed | tf_op | source)
XLA Modules:
  0.0 37.9 jit_solution(14283545651674451759)
XLA Ops:
  0.0 2.9 %collective-permute-start.6 = (bf16[2,4,96,512]{3,2,1,0:T(8,128)(2,1)}, bf16[2,4,96,512]{3,2,1,0:T(8,128)(2,1)S(1)}, u32[]{:S(2)}, u32[]{:S(2)}) collective-permute-start(bf16[2,4,96,512]{3,2,1,0:T(8,128)(2,1)} %own_ref.3), channel_id=1, source_target_pairs={{0,4},{4,8},{8,12},{1,5},{5,9},{9,13},{2,6},{6,10},{10,14},{3,7},{... | collective-permute-start | bytes 2359304 | tf_op jit(solution)/shard_map/ppermute | solution.py:80
  2.9 1.3 %stats.1 = (f32[8,128]{1,0:T(8,128)S(1)}, bf16[2,96,512]{2,1,0:T(8,128)(2,1)S(1)}, bf16[2,96,512]{2,1,0:T(8,128)(2,1)S(1)}) custom-call(bf16[2,4,96,512]{3,2,1,0:T(8,128)(2,1)} %own_ref.3), custom_call_target="tpu_custom_call" | custom-call | flops 20000000000 | bytes 786432 | tf_op jit(solution)/shard_map/stats/pallas_call | solution.py:47
  4.2 2.5 %collective-permute-start.4 = (bf16[2,96,512]{2,1,0:T(8,128)(2,1)S(1)}, bf16[2,96,512]{2,1,0:T(8,128)(2,1)S(1)}, u32[]{:S(2)}, u32[]{:S(2)}) collective-permute-start(bf16[2,96,512]{2,1,0:T(8,128)(2,1)S(1)} %get-tuple-element.11), channel_id=1, source_target_pairs={{0,1},{2,3},{1,0},{3,2},{4,5},{6,7},{5,4},{7,6},{8,9},{10,11},{9,8... | collective-permute-start | bytes 589832 | tf_op jit(solution)/shard_map/ppermute | solution.py:85
  6.7 0.7 %collective-permute-start.5 = (bf16[2,96,512]{2,1,0:T(8,128)(2,1)S(1)}, bf16[2,96,512]{2,1,0:T(8,128)(2,1)S(1)}, u32[]{:S(2)}, u32[]{:S(2)}) collective-permute-start(bf16[2,96,512]{2,1,0:T(8,128)(2,1)S(1)} %get-tuple-element.12), channel_id=1, source_target_pairs={{1,2},{2,1},{5,6},{6,5},{9,10},{10,9},{13,14},{14,13},{17,18},{18,... | collective-permute-start | bytes 589832 | tf_op jit(solution)/shard_map/ppermute | solution.py:85
  7.4 4.1 %collective-permute-done.4.edge_a_ref = bf16[2,96,512]{2,1,0:T(8,128)(2,1)S(1)} collective-permute-done((bf16[2,96,512]{2,1,0:T(8,128)(2,1)S(1)}, bf16[2,96,512]{2,1,0:T(8,128)(2,1)S(1)}, u32[]{:S(2)}, u32[]{:S(2)}) %collective-permute-start.4) | collective-permute-done | bytes 196640 | tf_op jit(solution)/shard_map/ppermute | solution.py:85
  11.5 0.0 collective-permute-done.5.edge_b_ref
  11.5 2.8 %collective-permute-start.7 = (bf16[4,96,512]{2,1,0:T(8,128)(2,1)S(1)}, bf16[4,96,512]{2,1,0:T(8,128)(2,1)S(1)}, u32[]{:S(2)}, u32[]{:S(2)}) collective-permute-start(bf16[4,96,512]{2,1,0:T(8,128)(2,1)S(1)} %pad_maximum_fusion), channel_id=1, source_target_pairs={{0,4},{4,8},{8,12},{1,5},{5,9},{9,13},{2,6},{6,10},{10,14},{3,7},{... | collective-permute-start | bytes 1179656 | tf_op jit(solution)/shard_map/ppermute | solution.py:80
  14.3 1.2 %collective-permute-start = (f32[8,128]{1,0:T(8,128)S(1)}, f32[8,128]{1,0:T(8,128)S(1)}, u32[]{:S(2)}, u32[]{:S(2)}) collective-permute-start(f32[8,128]{1,0:T(8,128)S(1)} %get-tuple-element.10), channel_id=1, source_target_pairs={{0,4},{4,0},{8,12},{12,8},{1,5},{5,1},{9,13},{13,9},{2,6},{6,2},{1... | collective-permute-start | bytes 12296 | tf_op jit(solution)/shard_map/ppermute | solution.py:75
  15.5 0.8 %collective-permute-done = f32[8,128]{1,0:T(8,128)S(1)} collective-permute-done((f32[8,128]{1,0:T(8,128)S(1)}, f32[8,128]{1,0:T(8,128)S(1)}, u32[]{:S(2)}, u32[]{:S(2)}) %collective-permute-start) | collective-permute-done | bytes 4128 | tf_op jit(solution)/shard_map/ppermute | solution.py:75
  16.3 0.3 collective-permute-start.1
  16.6 3.3 %collective-permute-done.1 = f32[8,128]{1,0:T(8,128)S(1)} collective-permute-done((f32[8,128]{1,0:T(8,128)S(1)}, f32[8,128]{1,0:T(8,128)S(1)}, u32[]{:S(2)}, u32[]{:S(2)}) %collective-permute-start.1) | collective-permute-done | bytes 4128 | tf_op jit(solution)/shard_map/ppermute | solution.py:75
  19.9 4.6 %collective-permute-start.2 = (f32[8,128]{1,0:T(8,128)S(1)}, f32[8,128]{1,0:T(8,128)S(1)}, u32[]{:S(2)}, u32[]{:S(2)}) collective-permute-start(f32[8,128]{1,0:T(8,128)S(1)} %add.13), channel_id=1, source_target_pairs={{0,1},{1,0},{2,3},{3,2},{4,5},{5,4},{6,7},{7,6},{8,9},{9,8},{10,11... | collective-permute-start | bytes 12296 | tf_op jit(solution)/shard_map/ppermute | solution.py:75
  24.5 1.6 %collective-permute-done.2 = f32[8,128]{1,0:T(8,128)S(1)} collective-permute-done((f32[8,128]{1,0:T(8,128)S(1)}, f32[8,128]{1,0:T(8,128)S(1)}, u32[]{:S(2)}, u32[]{:S(2)}) %collective-permute-start.2) | collective-permute-done | bytes 4128 | tf_op jit(solution)/shard_map/ppermute | solution.py:75
  26.1 3.2 %collective-permute-start.3 = (f32[8,128]{1,0:T(8,128)S(1)}, f32[8,128]{1,0:T(8,128)S(1)}, u32[]{:S(2)}, u32[]{:S(2)}) collective-permute-start(f32[8,128]{1,0:T(8,128)S(1)} %add.14), channel_id=1, source_target_pairs={{0,2},{1,3},{2,0},{3,1},{4,6},{5,7},{6,4},{7,5},{8,10},{9,11},{10,... | collective-permute-start | bytes 12296 | tf_op jit(solution)/shard_map/ppermute | solution.py:75
  29.3 1.6 %collective-permute-done.3 = f32[8,128]{1,0:T(8,128)S(1)} collective-permute-done((f32[8,128]{1,0:T(8,128)S(1)}, f32[8,128]{1,0:T(8,128)S(1)}, u32[]{:S(2)}, u32[]{:S(2)}) %collective-permute-start.3) | collective-permute-done | bytes 4128 | tf_op jit(solution)/shard_map/ppermute | solution.py:75
  30.9 0.0 copy-done.1
  30.9 0.0 copy-done
  30.9 0.0 copy-done.4
  30.9 0.0 copy-done.3
  30.9 0.0 copy-done.2
  30.9 3.2 %own.1 = (f32[2,4,96,256]{3,2,1,0:T(8,128)S(1)}, f32[8,512]{1,0:T(8,128)S(1)}) custom-call(f32[8,128]{1,0:T(8,128)S(1)} %add.15.sums_ref, f32[4,128]{1,0:T(4,128)S(1)} %bitcast.3, f32[4,128]{1,0:T(4,128)S(1)} %bitcast.4, f32[1,256]{1,0:T(1,128)S(1)} %bitcast.5, bf16[2,4,96,512]{3,2,1,0:T(8,128)(2,1)S(1)} %copy-done.1, ...), custom_call_target="tpu_custom_call" | custom-call | tf_op jit(solution)/shard_map/own/pallas_call | solution.py:257
  34.2 0.0 collective-permute-done.7.corners_ref
  34.2 0.0 collective-permute-done.6.earlier_ref
  34.2 3.7 %earlier.1 = bf16[2,4,96,256]{3,2,1,0:T(8,128)(2,1)} custom-call(f32[8,512]{1,0:T(8,128)S(1)} %get-tuple-element.13.coef, f32[2,4,96,256]{3,2,1,0:T(8,128)S(1)} %get-tuple-element.14.partial_ref, bf16[2,4,96,512]{3,2,1,0:T(8,128)(2,1)S(1)} %copy-done.1, bf16[2,96,512]{2,1,0:T(8,128)(2,1)S(1)} %collective-permute-done.4.edge_a_ref, ...), custom_call_target="tpu_custom_call" | custom-call | tf_op jit(solution)/shard_map/earlier/pallas_call | solution.py:278
  (10 shorter events, 0.1 us)
Async XLA Ops:
  0.0 30.9 %copy-start.1 = (bf16[2,4,96,512]{3,2,1,0:T(8,128)(2,1)S(1)}, bf16[2,4,96,512]{3,2,1,0:T(8,128)(2,1)}, u32[]{:S(2)}) copy-start(bf16[2,4,96,512]{3,2,1,0:T(8,128)(2,1)} %own_ref.3) | copy-start | bytes 2359300
  0.0 30.9 %copy-start = (bf16[3,3,3,512,256]{4,3,2,1,0:T(8,128)(2,1)S(1)}, bf16[3,3,3,512,256]{4,3,2,1,0:T(8,128)(2,1)}, u32[]{:S(2)}) copy-start(bf16[3,3,3,512,256]{4,3,2,1,0:T(8,128)(2,1)} %kernel_ref.3) | copy-start | bytes 21233668
  0.0 30.9 %copy-start.4 = (f32[256]{0:T(256)S(1)}, f32[256]{0:T(256)}, u32[]{:S(2)}) copy-start(f32[256]{0:T(256)} %param.9) | copy-start | bytes 3076
  0.0 30.9 %copy-start.3 = (f32[512]{0:T(512)S(1)}, f32[512]{0:T(512)}, u32[]{:S(2)}) copy-start(f32[512]{0:T(512)} %param.7) | copy-start | bytes 6148
  0.0 30.9 %copy-start.2 = (f32[512]{0:T(512)S(1)}, f32[512]{0:T(512)}, u32[]{:S(2)}) copy-start(f32[512]{0:T(512)} %param.6) | copy-start | bytes 6148
  0.0 34.2 %collective-permute-start.6 = (bf16[2,4,96,512]{3,2,1,0:T(8,128)(2,1)}, bf16[2,4,96,512]{3,2,1,0:T(8,128)(2,1)S(1)}, u32[]{:S(2)}, u32[]{:S(2)}) collective-permute-start(bf16[2,4,96,512]{3,2,1,0:T(8,128)(2,1)} %own_ref.3), channel_id=1, source_target_pairs={{0,4},{4,8},{8,12},{1,5},{5,9},{9,13},{2,6},{6,10},{10,14},{3,7},{... | collective-permute-start | bytes 2359304 | tf_op jit(solution)/shard_map/ppermute | solution.py:80
  4.2 7.3 %collective-permute-start.4 = (bf16[2,96,512]{2,1,0:T(8,128)(2,1)S(1)}, bf16[2,96,512]{2,1,0:T(8,128)(2,1)S(1)}, u32[]{:S(2)}, u32[]{:S(2)}) collective-permute-start(bf16[2,96,512]{2,1,0:T(8,128)(2,1)S(1)} %get-tuple-element.11), channel_id=1, source_target_pairs={{0,1},{2,3},{1,0},{3,2},{4,5},{6,7},{5,4},{7,6},{8,9},{10,11},{9,8... | collective-permute-start | bytes 589832 | tf_op jit(solution)/shard_map/ppermute | solution.py:85
  6.7 4.7 %collective-permute-start.5 = (bf16[2,96,512]{2,1,0:T(8,128)(2,1)S(1)}, bf16[2,96,512]{2,1,0:T(8,128)(2,1)S(1)}, u32[]{:S(2)}, u32[]{:S(2)}) collective-permute-start(bf16[2,96,512]{2,1,0:T(8,128)(2,1)S(1)} %get-tuple-element.12), channel_id=1, source_target_pairs={{1,2},{2,1},{5,6},{6,5},{9,10},{10,9},{13,14},{14,13},{17,18},{18,... | collective-permute-start | bytes 589832 | tf_op jit(solution)/shard_map/ppermute | solution.py:85
  11.5 22.7 %collective-permute-start.7 = (bf16[4,96,512]{2,1,0:T(8,128)(2,1)S(1)}, bf16[4,96,512]{2,1,0:T(8,128)(2,1)S(1)}, u32[]{:S(2)}, u32[]{:S(2)}) collective-permute-start(bf16[4,96,512]{2,1,0:T(8,128)(2,1)S(1)} %pad_maximum_fusion), channel_id=1, source_target_pairs={{0,4},{4,8},{8,12},{1,5},{5,9},{9,13},{2,6},{6,10},{10,14},{3,7},{... | collective-permute-start | bytes 1179656 | tf_op jit(solution)/shard_map/ppermute | solution.py:80
  14.3 2.0 %collective-permute-start = (f32[8,128]{1,0:T(8,128)S(1)}, f32[8,128]{1,0:T(8,128)S(1)}, u32[]{:S(2)}, u32[]{:S(2)}) collective-permute-start(f32[8,128]{1,0:T(8,128)S(1)} %get-tuple-element.10), channel_id=1, source_target_pairs={{0,4},{4,0},{8,12},{12,8},{1,5},{5,1},{9,13},{13,9},{2,6},{6,2},{1... | collective-permute-start | bytes 12296 | tf_op jit(solution)/shard_map/ppermute | solution.py:75
  16.3 3.6 %collective-permute-start.1 = (f32[8,128]{1,0:T(8,128)S(1)}, f32[8,128]{1,0:T(8,128)S(1)}, u32[]{:S(2)}, u32[]{:S(2)}) collective-permute-start(f32[8,128]{1,0:T(8,128)S(1)} %add.12), channel_id=1, source_target_pairs={{0,8},{4,12},{8,0},{12,4},{1,9},{5,13},{9,1},{13,5},{2,10},{6,14},... | collective-permute-start | bytes 12296 | tf_op jit(solution)/shard_map/ppermute | solution.py:75
  19.9 6.2 %collective-permute-start.2 = (f32[8,128]{1,0:T(8,128)S(1)}, f32[8,128]{1,0:T(8,128)S(1)}, u32[]{:S(2)}, u32[]{:S(2)}) collective-permute-start(f32[8,128]{1,0:T(8,128)S(1)} %add.13), channel_id=1, source_target_pairs={{0,1},{1,0},{2,3},{3,2},{4,5},{5,4},{6,7},{7,6},{8,9},{9,8},{10,11... | collective-permute-start | bytes 12296 | tf_op jit(solution)/shard_map/ppermute | solution.py:75
  26.1 4.8 %collective-permute-start.3 = (f32[8,128]{1,0:T(8,128)S(1)}, f32[8,128]{1,0:T(8,128)S(1)}, u32[]{:S(2)}, u32[]{:S(2)}) collective-permute-start(f32[8,128]{1,0:T(8,128)S(1)} %add.14), channel_id=1, source_target_pairs={{0,2},{1,3},{2,0},{3,1},{4,6},{5,7},{6,4},{7,5},{8,10},{9,11},{10,... | collective-permute-start | bytes 12296 | tf_op jit(solution)/shard_map/ppermute | solution.py:75
